TPU v7x, 32 devices: a whole 2x2x4 slice. The times are simulated.
32 devices in a mesh: pz: 4 (over z), py: 2 (over y), px: 4 (over x, core).
Axes of the slice: x: 2, y: 2, z: 4, core: 2. Of those that a mesh axis runs over, the one named last changes fastest.
Arguments:
- shift_diag: float32 [2, 320, 160, 192], P(None, 'px', 'py', 'pz')
- rhs_field: float32 [2, 320, 160, 192], P(None, 'px', 'py', 'pz')
- x_start: float32 [2, 320, 160, 192], P(None, 'px', 'py', 'pz')
- cond_x: float32 [2, 320, 160, 192], P(None, 'px', 'py', 'pz')
- cond_y: float32 [2, 320, 160, 192], P(None, 'px', 'py', 'pz')
- cond_z: float32 [2, 320, 160, 192], P(None, 'px', 'py', 'pz')
Outputs:
- output 1: float32 [2, 320, 160, 192], P(None, 'px', 'py', 'pz')
- output 2: float32 [2, 21], replicated
All inputs are finite; a program needn't handle non-finite values.
Results may differ from a plain program's by a relative error of at most 0.001.
Values sent between devices are 32-bit elements.
A program may use at most 1 GiB of HBM per device.

v0:
```python
import jax
import jax.numpy as jnp
from jax import lax
from jax.sharding import PartitionSpec as P

ITERS = 20
GRID_AXES = ('px', 'py', 'pz')
ALL_AXES = ('pz', 'py', 'px')


def up_pairs(axis_size):
    return [(dev_idx, dev_idx + 1) for dev_idx in range(axis_size - 1)]


def down_pairs(axis_size):
    return [(dev_idx, dev_idx - 1) for dev_idx in range(1, axis_size)]


def neighbour_planes(field, axis_name, axis_dim, axis_size):
    planes = field.shape[axis_dim]
    first_plane = lax.slice_in_dim(field, 0, 1, axis=axis_dim)
    last_plane = lax.slice_in_dim(field, planes - 1, planes, axis=axis_dim)
    from_below = lax.ppermute(last_plane, axis_name, up_pairs(axis_size))
    from_above = lax.ppermute(first_plane, axis_name, down_pairs(axis_size))
    return from_below, from_above


def extend_conduct(conduct, axis_name, axis_dim, axis_size):
    planes = conduct.shape[axis_dim]
    plane_index = lax.broadcasted_iota(jnp.int32, tuple(planes if pos_dim == axis_dim else 1 for pos_dim in range(conduct.ndim)), axis_dim)
    at_edge = jnp.logical_and(lax.axis_index(axis_name) == axis_size - 1, plane_index == planes - 1)
    masked = jnp.where(at_edge, 0.0, conduct)
    lower_faces = lax.ppermute(lax.slice_in_dim(conduct, planes - 1, planes, axis=axis_dim), axis_name, up_pairs(axis_size))
    return jnp.concatenate([lower_faces, masked], axis=axis_dim)


def apply_local(field, shift_diag, cond_ext, axis_sizes):
    halo_pairs = [neighbour_planes(field, GRID_AXES[axis_pos], axis_pos + 1, axis_sizes[axis_pos]) for axis_pos in range(3)]
    result = shift_diag * field
    for axis_pos in range(3):
        axis_dim = axis_pos + 1
        planes = field.shape[axis_dim]
        padded = jnp.concatenate([halo_pairs[axis_pos][0], field, halo_pairs[axis_pos][1]], axis=axis_dim)
        face_flux = cond_ext[axis_pos] * (lax.slice_in_dim(padded, 0, planes + 1, axis=axis_dim) - lax.slice_in_dim(padded, 1, planes + 2, axis=axis_dim))
        result = result + (lax.slice_in_dim(face_flux, 1, planes + 1, axis=axis_dim) - lax.slice_in_dim(face_flux, 0, planes, axis=axis_dim))
    return result


def solution(mesh):
    axis_sizes = tuple(mesh.shape[axis_name] for axis_name in GRID_AXES)
    field_spec = P(None, 'px', 'py', 'pz')

    def local_solve(shift_diag, rhs_field, x_start, cond_x, cond_y, cond_z):
        cell_count = x_start.shape[1] * x_start.shape[2] * x_start.shape[3] * axis_sizes[0] * axis_sizes[1] * axis_sizes[2]
        cond_ext = [extend_conduct(conduct, GRID_AXES[axis_pos], axis_pos + 1, axis_sizes[axis_pos]) for axis_pos, conduct in enumerate((cond_x, cond_y, cond_z))]

        def global_dot(left_vec, right_vec):
            return lax.psum(jnp.sum(left_vec * right_vec, axis=(1, 2, 3)), ALL_AXES)

        residual = rhs_field - apply_local(x_start, shift_diag, cond_ext, axis_sizes)
        rho_start = global_dot(residual, residual)

        def cg_step(loop_state, unused):
            x_cur, res_cur, direction, rho_old, beta_coef = loop_state
            direction = res_cur + beta_coef[:, None, None, None] * direction
            q_vec = apply_local(direction, shift_diag, cond_ext, axis_sizes)
            alpha_step = rho_old / global_dot(direction, q_vec)
            x_cur = x_cur + alpha_step[:, None, None, None] * direction
            res_cur = res_cur - alpha_step[:, None, None, None] * q_vec
            rho_new = global_dot(res_cur, res_cur)
            return (x_cur, res_cur, direction, rho_new, rho_new / rho_old), jnp.sqrt(rho_new / cell_count)

        init_state = (x_start, residual, jnp.zeros_like(residual), rho_start, jnp.zeros_like(rho_start))
        final_state, res_tail = lax.scan(cg_step, init_state, None, length=ITERS)
        res_hist = jnp.concatenate([jnp.sqrt(rho_start / cell_count)[None], res_tail], axis=0).T
        return final_state[0], res_hist

    return jax.shard_map(local_solve, mesh=mesh, in_specs=(field_spec, field_spec, field_spec, field_spec, field_spec, field_spec), out_specs=(field_spec, P(None, None)), check_vma=False)
```

profile of v0, /device:TPU:0, one launch (start us, length us, event | category | flops | bytes accessed | tf_op | source)
XLA Modules:
  0.0 3309.6 jit_solution(7681771072219256029)
XLA Ops:
  98.0 39.5 %psum.21 = f32[2]{0:T(128)} all-reduce(f32[2]{0:T(128)S(1)} %get-tuple-element.137), channel_id=1, replica_groups=mesh['pz'=4,'py'=2,'px'=4] {'pz','py','px'}, use_global_device_ids=true, to_apply=%region_1.2 | all-reduce | flops 2 | bytes 16 | tf_op jit(solution)/shard_map/psum | solution.py:58
  138.8 3170.0 %while.21 = (s32[]{:T(128)}, f32[2,80,80,48]{2,3,1,0:T(8,128)}, f32[2,80,80,48]{2,3,1,0:T(8,128)}, f32[2,80,80,48]{2,3,1,0:T(8,128)}, f32[2]{0:T(128)}, /*index=...) while((s32[]{:T(128)}, f32[2,80,80,48]{2,3,1,0:T(8,128)}, ...), condition=%wide.region_7.8_spmd.clone, body=%wide.region_2.7_spmd.clone.sunk | while | flops 18544652 | bytes 88187488 | solution.py:74
  199.4 44.9 %psum.26 = f32[2]{0:T(128)S(1)} all-reduce(f32[2]{0:T(128)S(1)} %get-tuple-element.247), channel_id=1, replica_groups=mesh['pz'=4,'py'=2,'px'=4] {'pz','py','px'}, use_global_device_ids=true, to_apply=%region_4.4 | all-reduce | flops 2 | bytes 16 | tf_op jit(solution)/shard_map/while/body/eval_jaxpr/psum | solution.py:58
  244.9 9.5 multiply_reduce_fusion.6
  254.4 39.9 %psum.27 = f32[2]{0:T(128)S(1)} all-reduce(f32[2]{0:T(128)S(1)} %get-tuple-element.250), channel_id=1, replica_groups=mesh['pz'=4,'py'=2,'px'=4] {'pz','py','px'}, use_global_device_ids=true, to_apply=%region_6.6 | all-reduce | flops 2 | bytes 16 | tf_op jit(solution)/shard_map/while/body/eval_jaxpr/psum | solution.py:58
  357.1 45.8 %psum.26 = f32[2]{0:T(128)S(1)} all-reduce(f32[2]{0:T(128)S(1)} %get-tuple-element.247), channel_id=1, replica_groups=mesh['pz'=4,'py'=2,'px'=4] {'pz','py','px'}, use_global_device_ids=true, to_apply=%region_4.4 | all-reduce | flops 2 | bytes 16 | tf_op jit(solution)/shard_map/while/body/eval_jaxpr/psum | solution.py:58
  403.5 9.5 multiply_reduce_fusion.6
  413.0 39.9 %psum.27 = f32[2]{0:T(128)S(1)} all-reduce(f32[2]{0:T(128)S(1)} %get-tuple-element.250), channel_id=1, replica_groups=mesh['pz'=4,'py'=2,'px'=4] {'pz','py','px'}, use_global_device_ids=true, to_apply=%region_6.6 | all-reduce | flops 2 | bytes 16 | tf_op jit(solution)/shard_map/while/body/eval_jaxpr/psum | solution.py:58
  459.8 7.6 fusion.32
  515.7 45.8 %psum.26 = f32[2]{0:T(128)S(1)} all-reduce(f32[2]{0:T(128)S(1)} %get-tuple-element.247), channel_id=1, replica_groups=mesh['pz'=4,'py'=2,'px'=4] {'pz','py','px'}, use_global_device_ids=true, to_apply=%region_4.4 | all-reduce | flops 2 | bytes 16 | tf_op jit(solution)/shard_map/while/body/eval_jaxpr/psum | solution.py:58
  562.1 9.5 multiply_reduce_fusion.6
  571.6 39.9 %psum.27 = f32[2]{0:T(128)S(1)} all-reduce(f32[2]{0:T(128)S(1)} %get-tuple-element.250), channel_id=1, replica_groups=mesh['pz'=4,'py'=2,'px'=4] {'pz','py','px'}, use_global_device_ids=true, to_apply=%region_6.6 | all-reduce | flops 2 | bytes 16 | tf_op jit(solution)/shard_map/while/body/eval_jaxpr/psum | solution.py:58
  618.4 7.6 fusion.32
  674.3 45.8 %psum.26 = f32[2]{0:T(128)S(1)} all-reduce(f32[2]{0:T(128)S(1)} %get-tuple-element.247), channel_id=1, replica_groups=mesh['pz'=4,'py'=2,'px'=4] {'pz','py','px'}, use_global_device_ids=true, to_apply=%region_4.4 | all-reduce | flops 2 | bytes 16 | tf_op jit(solution)/shard_map/while/body/eval_jaxpr/psum | solution.py:58
  720.7 9.5 multiply_reduce_fusion.6
  730.2 39.9 %psum.27 = f32[2]{0:T(128)S(1)} all-reduce(f32[2]{0:T(128)S(1)} %get-tuple-element.250), channel_id=1, replica_groups=mesh['pz'=4,'py'=2,'px'=4] {'pz','py','px'}, use_global_device_ids=true, to_apply=%region_6.6 | all-reduce | flops 2 | bytes 16 | tf_op jit(solution)/shard_map/while/body/eval_jaxpr/psum | solution.py:58
  832.9 45.8 %psum.26 = f32[2]{0:T(128)S(1)} all-reduce(f32[2]{0:T(128)S(1)} %get-tuple-element.247), channel_id=1, replica_groups=mesh['pz'=4,'py'=2,'px'=4] {'pz','py','px'}, use_global_device_ids=true, to_apply=%region_4.4 | all-reduce | flops 2 | bytes 16 | tf_op jit(solution)/shard_map/while/body/eval_jaxpr/psum | solution.py:58
  879.3 9.5 multiply_reduce_fusion.6
  888.8 39.9 %psum.27 = f32[2]{0:T(128)S(1)} all-reduce(f32[2]{0:T(128)S(1)} %get-tuple-element.250), channel_id=1, replica_groups=mesh['pz'=4,'py'=2,'px'=4] {'pz','py','px'}, use_global_device_ids=true, to_apply=%region_6.6 | all-reduce | flops 2 | bytes 16 | tf_op jit(solution)/shard_map/while/body/eval_jaxpr/psum | solution.py:58
  991.5 45.8 %psum.26 = f32[2]{0:T(128)S(1)} all-reduce(f32[2]{0:T(128)S(1)} %get-tuple-element.247), channel_id=1, replica_groups=mesh['pz'=4,'py'=2,'px'=4] {'pz','py','px'}, use_global_device_ids=true, to_apply=%region_4.4 | all-reduce | flops 2 | bytes 16 | tf_op jit(solution)/shard_map/while/body/eval_jaxpr/psum | solution.py:58
  1037.9 9.5 multiply_reduce_fusion.6
  1047.4 39.9 %psum.27 = f32[2]{0:T(128)S(1)} all-reduce(f32[2]{0:T(128)S(1)} %get-tuple-element.250), channel_id=1, replica_groups=mesh['pz'=4,'py'=2,'px'=4] {'pz','py','px'}, use_global_device_ids=true, to_apply=%region_6.6 | all-reduce | flops 2 | bytes 16 | tf_op jit(solution)/shard_map/while/body/eval_jaxpr/psum | solution.py:58
  1150.1 45.8 %psum.26 = f32[2]{0:T(128)S(1)} all-reduce(f32[2]{0:T(128)S(1)} %get-tuple-element.247), channel_id=1, replica_groups=mesh['pz'=4,'py'=2,'px'=4] {'pz','py','px'}, use_global_device_ids=true, to_apply=%region_4.4 | all-reduce | flops 2 | bytes 16 | tf_op jit(solution)/shard_map/while/body/eval_jaxpr/psum | solution.py:58
  1196.5 9.5 multiply_reduce_fusion.6
  1206.0 39.9 %psum.27 = f32[2]{0:T(128)S(1)} all-reduce(f32[2]{0:T(128)S(1)} %get-tuple-element.250), channel_id=1, replica_groups=mesh['pz'=4,'py'=2,'px'=4] {'pz','py','px'}, use_global_device_ids=true, to_apply=%region_6.6 | all-reduce | flops 2 | bytes 16 | tf_op jit(solution)/shard_map/while/body/eval_jaxpr/psum | solution.py:58
  1308.7 45.8 %psum.26 = f32[2]{0:T(128)S(1)} all-reduce(f32[2]{0:T(128)S(1)} %get-tuple-element.247), channel_id=1, replica_groups=mesh['pz'=4,'py'=2,'px'=4] {'pz','py','px'}, use_global_device_ids=true, to_apply=%region_4.4 | all-reduce | flops 2 | bytes 16 | tf_op jit(solution)/shard_map/while/body/eval_jaxpr/psum | solution.py:58
  1355.1 9.5 multiply_reduce_fusion.6
  1364.6 39.9 %psum.27 = f32[2]{0:T(128)S(1)} all-reduce(f32[2]{0:T(128)S(1)} %get-tuple-element.250), channel_id=1, replica_groups=mesh['pz'=4,'py'=2,'px'=4] {'pz','py','px'}, use_global_device_ids=true, to_apply=%region_6.6 | all-reduce | flops 2 | bytes 16 | tf_op jit(solution)/shard_map/while/body/eval_jaxpr/psum | solution.py:58
  1467.3 45.8 %psum.26 = f32[2]{0:T(128)S(1)} all-reduce(f32[2]{0:T(128)S(1)} %get-tuple-element.247), channel_id=1, replica_groups=mesh['pz'=4,'py'=2,'px'=4] {'pz','py','px'}, use_global_device_ids=true, to_apply=%region_4.4 | all-reduce | flops 2 | bytes 16 | tf_op jit(solution)/shard_map/while/body/eval_jaxpr/psum | solution.py:58
  1513.7 9.5 multiply_reduce_fusion.6
  1523.2 39.9 %psum.27 = f32[2]{0:T(128)S(1)} all-reduce(f32[2]{0:T(128)S(1)} %get-tuple-element.250), channel_id=1, replica_groups=mesh['pz'=4,'py'=2,'px'=4] {'pz','py','px'}, use_global_device_ids=true, to_apply=%region_6.6 | all-reduce | flops 2 | bytes 16 | tf_op jit(solution)/shard_map/while/body/eval_jaxpr/psum | solution.py:58
  1625.9 45.8 %psum.26 = f32[2]{0:T(128)S(1)} all-reduce(f32[2]{0:T(128)S(1)} %get-tuple-element.247), channel_id=1, replica_groups=mesh['pz'=4,'py'=2,'px'=4] {'pz','py','px'}, use_global_device_ids=true, to_apply=%region_4.4 | all-reduce | flops 2 | bytes 16 | tf_op jit(solution)/shard_map/while/body/eval_jaxpr/psum | solution.py:58
  1672.2 9.5 multiply_reduce_fusion.6
  1681.8 39.9 %psum.27 = f32[2]{0:T(128)S(1)} all-reduce(f32[2]{0:T(128)S(1)} %get-tuple-element.250), channel_id=1, replica_groups=mesh['pz'=4,'py'=2,'px'=4] {'pz','py','px'}, use_global_device_ids=true, to_apply=%region_6.6 | all-reduce | flops 2 | bytes 16 | tf_op jit(solution)/shard_map/while/body/eval_jaxpr/psum | solution.py:58
  1784.5 45.8 %psum.26 = f32[2]{0:T(128)S(1)} all-reduce(f32[2]{0:T(128)S(1)} %get-tuple-element.247), channel_id=1, replica_groups=mesh['pz'=4,'py'=2,'px'=4] {'pz','py','px'}, use_global_device_ids=true, to_apply=%region_4.4 | all-reduce | flops 2 | bytes 16 | tf_op jit(solution)/shard_map/while/body/eval_jaxpr/psum | solution.py:58
  1830.8 9.5 multiply_reduce_fusion.6
  1840.3 39.9 %psum.27 = f32[2]{0:T(128)S(1)} all-reduce(f32[2]{0:T(128)S(1)} %get-tuple-element.250), channel_id=1, replica_groups=mesh['pz'=4,'py'=2,'px'=4] {'pz','py','px'}, use_global_device_ids=true, to_apply=%region_6.6 | all-reduce | flops 2 | bytes 16 | tf_op jit(solution)/shard_map/while/body/eval_jaxpr/psum | solution.py:58
  1943.0 45.8 %psum.26 = f32[2]{0:T(128)S(1)} all-reduce(f32[2]{0:T(128)S(1)} %get-tuple-element.247), channel_id=1, replica_groups=mesh['pz'=4,'py'=2,'px'=4] {'pz','py','px'}, use_global_device_ids=true, to_apply=%region_4.4 | all-reduce | flops 2 | bytes 16 | tf_op jit(solution)/shard_map/while/body/eval_jaxpr/psum | solution.py:58
  1989.4 9.5 multiply_reduce_fusion.6
  1998.9 39.9 %psum.27 = f32[2]{0:T(128)S(1)} all-reduce(f32[2]{0:T(128)S(1)} %get-tuple-element.250), channel_id=1, replica_groups=mesh['pz'=4,'py'=2,'px'=4] {'pz','py','px'}, use_global_device_ids=true, to_apply=%region_6.6 | all-reduce | flops 2 | bytes 16 | tf_op jit(solution)/shard_map/while/body/eval_jaxpr/psum | solution.py:58
  2101.6 45.8 %psum.26 = f32[2]{0:T(128)S(1)} all-reduce(f32[2]{0:T(128)S(1)} %get-tuple-element.247), channel_id=1, replica_groups=mesh['pz'=4,'py'=2,'px'=4] {'pz','py','px'}, use_global_device_ids=true, to_apply=%region_4.4 | all-reduce | flops 2 | bytes 16 | tf_op jit(solution)/shard_map/while/body/eval_jaxpr/psum | solution.py:58
  2148.0 9.5 multiply_reduce_fusion.6
  2157.5 39.9 %psum.27 = f32[2]{0:T(128)S(1)} all-reduce(f32[2]{0:T(128)S(1)} %get-tuple-element.250), channel_id=1, replica_groups=mesh['pz'=4,'py'=2,'px'=4] {'pz','py','px'}, use_global_device_ids=true, to_apply=%region_6.6 | all-reduce | flops 2 | bytes 16 | tf_op jit(solution)/shard_map/while/body/eval_jaxpr/psum | solution.py:58
  2260.2 45.8 %psum.26 = f32[2]{0:T(128)S(1)} all-reduce(f32[2]{0:T(128)S(1)} %get-tuple-element.247), channel_id=1, replica_groups=mesh['pz'=4,'py'=2,'px'=4] {'pz','py','px'}, use_global_device_ids=true, to_apply=%region_4.4 | all-reduce | flops 2 | bytes 16 | tf_op jit(solution)/shard_map/while/body/eval_jaxpr/psum | solution.py:58
  2306.6 9.5 multiply_reduce_fusion.6
  2316.1 39.9 %psum.27 = f32[2]{0:T(128)S(1)} all-reduce(f32[2]{0:T(128)S(1)} %get-tuple-element.250), channel_id=1, replica_groups=mesh['pz'=4,'py'=2,'px'=4] {'pz','py','px'}, use_global_device_ids=true, to_apply=%region_6.6 | all-reduce | flops 2 | bytes 16 | tf_op jit(solution)/shard_map/while/body/eval_jaxpr/psum | solution.py:58
  2418.8 45.8 %psum.26 = f32[2]{0:T(128)S(1)} all-reduce(f32[2]{0:T(128)S(1)} %get-tuple-element.247), channel_id=1, replica_groups=mesh['pz'=4,'py'=2,'px'=4] {'pz','py','px'}, use_global_device_ids=true, to_apply=%region_4.4 | all-reduce | flops 2 | bytes 16 | tf_op jit(solution)/shard_map/while/body/eval_jaxpr/psum | solution.py:58
  2465.2 9.5 multiply_reduce_fusion.6
  2474.7 39.9 %psum.27 = f32[2]{0:T(128)S(1)} all-reduce(f32[2]{0:T(128)S(1)} %get-tuple-element.250), channel_id=1, replica_groups=mesh['pz'=4,'py'=2,'px'=4] {'pz','py','px'}, use_global_device_ids=true, to_apply=%region_6.6 | all-reduce | flops 2 | bytes 16 | tf_op jit(solution)/shard_map/while/body/eval_jaxpr/psum | solution.py:58
  2577.4 45.8 %psum.26 = f32[2]{0:T(128)S(1)} all-reduce(f32[2]{0:T(128)S(1)} %get-tuple-element.247), channel_id=1, replica_groups=mesh['pz'=4,'py'=2,'px'=4] {'pz','py','px'}, use_global_device_ids=true, to_apply=%region_4.4 | all-reduce | flops 2 | bytes 16 | tf_op jit(solution)/shard_map/while/body/eval_jaxpr/psum | solution.py:58
  2623.8 9.5 multiply_reduce_fusion.6
  2633.3 39.9 %psum.27 = f32[2]{0:T(128)S(1)} all-reduce(f32[2]{0:T(128)S(1)} %get-tuple-element.250), channel_id=1, replica_groups=mesh['pz'=4,'py'=2,'px'=4] {'pz','py','px'}, use_global_device_ids=true, to_apply=%region_6.6 | all-reduce | flops 2 | bytes 16 | tf_op jit(solution)/shard_map/while/body/eval_jaxpr/psum | solution.py:58
  2736.0 45.8 %psum.26 = f32[2]{0:T(128)S(1)} all-reduce(f32[2]{0:T(128)S(1)} %get-tuple-element.247), channel_id=1, replica_groups=mesh['pz'=4,'py'=2,'px'=4] {'pz','py','px'}, use_global_device_ids=true, to_apply=%region_4.4 | all-reduce | flops 2 | bytes 16 | tf_op jit(solution)/shard_map/while/body/eval_jaxpr/psum | solution.py:58
  2782.4 9.5 multiply_reduce_fusion.6
  2791.9 39.9 %psum.27 = f32[2]{0:T(128)S(1)} all-reduce(f32[2]{0:T(128)S(1)} %get-tuple-element.250), channel_id=1, replica_groups=mesh['pz'=4,'py'=2,'px'=4] {'pz','py','px'}, use_global_device_ids=true, to_apply=%region_6.6 | all-reduce | flops 2 | bytes 16 | tf_op jit(solution)/shard_map/while/body/eval_jaxpr/psum | solution.py:58
  2894.6 45.8 %psum.26 = f32[2]{0:T(128)S(1)} all-reduce(f32[2]{0:T(128)S(1)} %get-tuple-element.247), channel_id=1, replica_groups=mesh['pz'=4,'py'=2,'px'=4] {'pz','py','px'}, use_global_device_ids=true, to_apply=%region_4.4 | all-reduce | flops 2 | bytes 16 | tf_op jit(solution)/shard_map/while/body/eval_jaxpr/psum | solution.py:58
  2941.0 9.5 multiply_reduce_fusion.6
  2950.5 39.9 %psum.27 = f32[2]{0:T(128)S(1)} all-reduce(f32[2]{0:T(128)S(1)} %get-tuple-element.250), channel_id=1, replica_groups=mesh['pz'=4,'py'=2,'px'=4] {'pz','py','px'}, use_global_device_ids=true, to_apply=%region_6.6 | all-reduce | flops 2 | bytes 16 | tf_op jit(solution)/shard_map/while/body/eval_jaxpr/psum | solution.py:58
  3053.2 45.8 %psum.26 = f32[2]{0:T(128)S(1)} all-reduce(f32[2]{0:T(128)S(1)} %get-tuple-element.247), channel_id=1, replica_groups=mesh['pz'=4,'py'=2,'px'=4] {'pz','py','px'}, use_global_device_ids=true, to_apply=%region_4.4 | all-reduce | flops 2 | bytes 16 | tf_op jit(solution)/shard_map/while/body/eval_jaxpr/psum | solution.py:58
  3099.6 9.5 multiply_reduce_fusion.6
  3109.1 39.9 %psum.27 = f32[2]{0:T(128)S(1)} all-reduce(f32[2]{0:T(128)S(1)} %get-tuple-element.250), channel_id=1, replica_groups=mesh['pz'=4,'py'=2,'px'=4] {'pz','py','px'}, use_global_device_ids=true, to_apply=%region_6.6 | all-reduce | flops 2 | bytes 16 | tf_op jit(solution)/shard_map/while/body/eval_jaxpr/psum | solution.py:58
  3211.8 45.8 %psum.26 = f32[2]{0:T(128)S(1)} all-reduce(f32[2]{0:T(128)S(1)} %get-tuple-element.247), channel_id=1, replica_groups=mesh['pz'=4,'py'=2,'px'=4] {'pz','py','px'}, use_global_device_ids=true, to_apply=%region_4.4 | all-reduce | flops 2 | bytes 16 | tf_op jit(solution)/shard_map/while/body/eval_jaxpr/psum | solution.py:58
  3258.2 9.5 multiply_reduce_fusion.6
  3267.7 39.9 %psum.27 = f32[2]{0:T(128)S(1)} all-reduce(f32[2]{0:T(128)S(1)} %get-tuple-element.250), channel_id=1, replica_groups=mesh['pz'=4,'py'=2,'px'=4] {'pz','py','px'}, use_global_device_ids=true, to_apply=%region_6.6 | all-reduce | flops 2 | bytes 16 | tf_op jit(solution)/shard_map/while/body/eval_jaxpr/psum | solution.py:58
  (722 shorter events, 1347.8 us)
Async XLA Ops:
  10.2 37.2 %collective-permute-start.10 = (f32[2,80,1,48]{1,3,2,0:T(8,128)S(1)}, f32[2,80,1,48]{1,3,2,0:T(8,128)S(1)}, u32[]{:S(2)}, u32[]{:S(2)}) collective-permute-start(f32[2,80,1,48]{1,3,2,0:T(8,128)S(1)} %copy.66), channel_id=1, source_target_pairs={{0,4},{1,5},{2,6},{3,7},{8,12},{9,13},{10,14},{11,15},{16,20},{17,... | collective-permute-start | bytes 92168 | tf_op jit(solution)/shard_map/ppermute | solution.py:23
  18.1 39.0 %collective-permute-start.11 = (f32[2,80,1,48]{1,3,2,0:T(8,128)S(1)}, f32[2,80,1,48]{1,3,2,0:T(8,128)S(1)}, u32[]{:S(2)}, u32[]{:S(2)}) collective-permute-start(f32[2,80,1,48]{1,3,2,0:T(8,128)S(1)} %copy.67), channel_id=1, source_target_pairs={{4,0},{5,1},{6,2},{7,3},{12,8},{13,9},{14,10},{15,11},{20,16},{21,... | collective-permute-start | bytes 92168 | tf_op jit(solution)/shard_map/ppermute | solution.py:24
  27.5 35.9 %collective-permute-start.9 = (f32[2,80,1,48]{1,3,2,0:T(8,128)S(1)}, f32[2,80,1,48]{1,3,2,0:T(8,128)S(1)}, u32[]{:S(2)}, u32[]{:S(2)}) collective-permute-start(f32[2,80,1,48]{1,3,2,0:T(8,128)S(1)} %copy.65), channel_id=1, source_target_pairs={{0,4},{1,5},{2,6},{3,7},{8,12},{9,13},{10,14},{11,15},{16,20},{17,... | collective-permute-start | bytes 92168 | tf_op jit(solution)/shard_map/ppermute | solution.py:33
  32.9 34.7 %collective-permute-start.7 = (f32[2,1,80,48]{2,3,1,0:T(8,128)S(1)}, f32[2,1,80,48]{2,3,1,0:T(8,128)S(1)}, u32[]{:S(2)}, u32[]{:S(2)}) collective-permute-start(f32[2,1,80,48]{2,3,1,0:T(8,128)S(1)} %get-tuple-element.155), channel_id=1, source_target_pairs={{0,1},{1,2},{2,3},{4,5},{5,6},{6,7},{8,9},{9,10},{10,11},{12,13},{... | collective-permute-start | bytes 92168 | tf_op jit(solution)/shard_map/ppermute | solution.py:23
  46.1 26.3 collective-permute-start.8
  47.4 25.0 collective-permute-start.6
  59.9 26.1 collective-permute-start.13
  66.3 19.8 collective-permute-start.14
  67.6 18.5 collective-permute-start.12
  153.9 15.6 collective-permute-start.2
  167.4 22.8 collective-permute-start
  169.5 20.8 collective-permute-start.1
  311.9 15.3 collective-permute-start.2
  325.2 22.7 collective-permute-start
  327.2 20.8 collective-permute-start.1
  470.5 15.3 collective-permute-start.2
  483.8 22.7 collective-permute-start
  485.8 20.8 collective-permute-start.1
  629.1 15.3 collective-permute-start.2
  642.4 22.7 collective-permute-start
  644.4 20.8 collective-permute-start.1
  787.6 15.3 collective-permute-start.2
  801.0 22.7 collective-permute-start
  803.0 20.8 collective-permute-start.1
  946.2 15.3 collective-permute-start.2
  959.6 22.7 collective-permute-start
  961.6 20.8 collective-permute-start.1
  1104.8 15.3 collective-permute-start.2
  1118.2 22.7 collective-permute-start
  1120.1 20.8 collective-permute-start.1
  1276.7 22.7 collective-permute-start
  1278.7 20.8 collective-permute-start.1
  1435.3 22.7 collective-permute-start
  1437.3 20.8 collective-permute-start.1
  1580.6 15.3 collective-permute-start.2
  1593.9 22.7 collective-permute-start
  1595.9 20.8 collective-permute-start.1
  1739.2 15.3 collective-permute-start.2
  1752.5 22.7 collective-permute-start
  1754.5 20.8 collective-permute-start.1
  1897.8 15.3 collective-permute-start.2
  1911.1 22.7 collective-permute-start
  1913.1 20.8 collective-permute-start.1
  2069.7 22.7 collective-permute-start
  2071.7 20.8 collective-permute-start.1
  2228.3 22.7 collective-permute-start
  2230.3 20.8 collective-permute-start.1
  2373.6 15.3 collective-permute-start.2
  2386.9 22.7 collective-permute-start
  2388.9 20.8 collective-permute-start.1
  2532.2 15.3 collective-permute-start.2
  2545.5 22.7 collective-permute-start
  2547.5 20.8 collective-permute-start.1
  2690.8 15.3 collective-permute-start.2
  2704.1 22.7 collective-permute-start
  2706.1 20.8 collective-permute-start.1
  2862.7 22.7 collective-permute-start
  2864.7 20.8 collective-permute-start.1
  3008.0 15.3 collective-permute-start.2
  3021.3 22.7 collective-permute-start
  3023.3 20.8 collective-permute-start.1
  3166.6 15.3 collective-permute-start.2
  3179.9 22.7 collective-permute-start
  3181.9 20.8 collective-permute-start.1
  (113 other events, 4254.5 us)
where the time goes:
time: 3320 us; the launch traced here: 3310 us
  blocking collectives  1750 us (53%)
  other arithmetic  825 us (25%)
  local copies, waits for them, and re-layouts  473 us (14%)
  starting transfers between devices  254 us (8%)
    psum x41, blocking collectives, global_dot(): return lax.psum(jnp.sum(left_vec * right_vec, axis=(1, 2, 3)), ALL_AXES)  1750 us
    mul x61, other arithmetic, apply_local(): cond_ext[axis_pos]  355 us
    reduce_sum x41, other arithmetic, global_dot(): return lax.psum(jnp.sum(left_vec * right_vec, axis=(1, 2, 3)), ALL_AXES)  309 us
    slice x83, local copies, waits for them, and re-layouts, neighbour_planes(): first_plane = lax.slice_in_dim(field, 0, 1, axis=axis_dim)  265 us
    ppermute x63, starting transfers between devices, neighbour_planes(): from_below = lax.ppermute(last_plane, axis_name, up_pairs(axis_size))  158 us
    add x20, other arithmetic, cg_step(): direction = res_cur + beta_coef[:, None, None, None] * direction  113 us
    ppermute x63, starting transfers between devices, neighbour_planes(): from_above = lax.ppermute(first_plane, axis_name, down_pairs(axis_size))  81.2 us
  transfers between devices with their start and end apart: 129, of which 0 were waited for; matrix products, arithmetic and copies ran while one was open for 16% of the time, Pallas kernels for 0%

commit v1 on v0

v1 whole, which is shorter than its diff:
```python
import functools

import jax
import jax.numpy as jnp
from jax import lax
from jax.experimental import pallas as pl
from jax.experimental.pallas import tpu as pltpu
from jax.sharding import PartitionSpec as P

ITERS = 20
AXES = ('pz', 'py', 'px')
MESH = pl.DeviceIdType.MESH
XB, YB, ZB = 16, 8, 8


def kernel(sizes, dims, s_hbm, b_hbm, x_hbm, kx_hbm, ky_hbm, kz_hbm, xo_hbm, hist_ref,
           stage, r, p, q, x, s, kx, ky, kz, fx, tmp,
           xs, xr, ys, yr, zs, zr, kxs, kxr, kys, kyr, kzs, kzr,
           dots, rho, hist,
           in_sem, out_sem, dot_send, dot_recv, halo_send, halo_recv, k_send, k_recv):
    nz_dev, ny_dev, nx_dev = sizes
    n_dev = nz_dev * ny_dev * nx_dev
    XI, YI, ZI, cells = dims
    pz, py, px = (lax.axis_index(a) for a in AXES)
    me = (pz * ny_dev + py) * nx_dev + px
    lane = lax.broadcasted_iota(jnp.int32, (8, 128), 1)
    sub = lax.broadcasted_iota(jnp.int32, (8, 128), 0)
    lane_z = lax.rem(lane, ZB)
    lane_x = lax.div(lane, ZB)
    row_lane = lax.broadcasted_iota(jnp.int32, (1, 128), 1)

    arrays = (x_hbm, kx_hbm, ky_hbm, kz_hbm, s_hbm, b_hbm)

    def in_copy(a, c):
        return pltpu.make_async_copy(arrays[a].at[c], stage.at[a, c], in_sem.at[a, c])

    for a in range(6):
        for c in range(2):
            in_copy(a, c).start()

    for ref in (xr, yr, zr, kxr, kyr, kzr):
        ref[...] = jnp.zeros(ref.shape, ref.dtype)

    def target(off):
        t = lax.rem(me + off, n_dev)
        rest = lax.rem(t, ny_dev * nx_dev)
        return (lax.div(t, ny_dev * nx_dev), lax.div(rest, nx_dev), lax.rem(rest, nx_dev))

    def each_other(fn):
        def step(i, _):
            fn(target(i))
            return 0
        lax.fori_loop(1, n_dev, step, 0, unroll=True)

    barrier = pltpu.get_barrier_semaphore()
    each_other(lambda dev: pl.semaphore_signal(barrier, inc=1, device_id=dev, device_id_type=MESH))
    pl.semaphore_wait(barrier, n_dev - 1)

    def unrolled(n, fn):
        def step(i, _):
            fn(i)
            return 0
        lax.fori_loop(0, n, step, 0, unroll=True)

    ysl, zsl = slice(1, YI + 1), slice(1, ZI + 1)
    xsl = slice(1, XI + 1)

    def relayout(a, stores):
        def system(c, _):
            in_copy(a, c).wait()

            def plane(xi, _):
                def load(zi):
                    rows = stage[a, c, :, xi, pl.ds(zi, ZB, stride=ZI), :]
                    tmp[zi] = rows.reshape(128, rows.shape[-1]).T
                unrolled(ZI, load)
                unrolled(ZI, lambda zi: unrolled(YI, lambda yi: stores(c, xi, yi, zi, tmp[zi, pl.ds(yi, YB, stride=YI), :])))
                return 0
            return lax.fori_loop(0, XI, plane, 0)
        lax.fori_loop(0, 2, system, 0)

    def pack_x(get, shift, put):
        acc = pltpu.roll(get(0), shift, 2) if shift else get(0)
        for j in range(1, YI):
            acc = jnp.where(lane_x == j, pltpu.roll(get(j), (shift + ZB * j) % 128, 2), acc)
        put(acc)

    def pack_z(get, src_zb, put):
        acc = pltpu.roll(get(0), (-src_zb) % 128, 2) if src_zb else get(0)
        for j in range(1, XI):
            v = get(j)
            acc = jnp.where(lane_z == j, pltpu.roll(v, (j - src_zb) % 128, 2) if j != src_zb else v, acc)
        put(acc)

    def ghost_x(v, packed, j, low):
        dst = 0 if low else XB - 1
        moved = pltpu.roll(v, ZB if low else 128 - ZB, 2)
        move = (ZB * (dst - j)) % 128
        return jnp.where(lane_x == dst, pltpu.roll(packed, move, 2) if move else packed, moved)

    def ghost_z(v, packed, j, low):
        dst = 0 if low else ZB - 1
        moved = pltpu.roll(v, 1 if low else 127, 2)
        move = (dst - j) % 128
        return jnp.where(lane_z == dst, pltpu.roll(packed, move, 2) if move else packed, moved)

    def ghost_y(v, rows, low):
        dst = 0 if low else YB - 1
        moved = pltpu.roll(v, 1 if low else YB - 1, v.ndim - 2)
        return jnp.where(sub == dst, jnp.broadcast_to(rows, v.shape), moved)

    def pack_field(f, c):
        def put(ref, d):
            def put_(v):
                ref[d, c] = v
            return put_
        pack_x(lambda yi: f[c, 1, yi + 1, zsl], 0, put(xs, 0))
        pack_x(lambda yi: f[c, XI, yi + 1, zsl], ZB, put(xs, 1))
        pack_z(lambda xi: f[c, xi + 1, ysl, 1], 0, put(zs, 0))
        pack_z(lambda xi: f[c, xi + 1, ysl, ZI], ZB - 1, put(zs, 1))
        ys[0, c] = f[c, xsl, 1, zsl, 0:1, :]
        ys[1, c] = f[c, xsl, YI, zsl, YB - 1:YB, :]

    def ghost_field(f, c, w):
        for yi in range(YI):
            f[c, 0, yi + 1, zsl] = ghost_x(f[c, XI, yi + 1, zsl], xr[w, 0, c], yi, True)
            f[c, XI + 1, yi + 1, zsl] = ghost_x(f[c, 1, yi + 1, zsl], xr[w, 1, c], yi, False)
        for xi in range(XI):
            f[c, xi + 1, ysl, 0] = ghost_z(f[c, xi + 1, ysl, ZI], zr[w, 0, c], xi, True)
            f[c, xi + 1, ysl, ZI + 1] = ghost_z(f[c, xi + 1, ysl, 1], zr[w, 1, c], xi, False)
        f[c, xsl, 0, zsl] = ghost_y(f[c, xsl, YI, zsl], yr[w, 0, c], True)
        f[c, xsl, YI + 1, zsl] = ghost_y(f[c, xsl, 1, zsl], yr[w, 1, c], False)

    lower = ((px > 0, (pz, py, px - 1)), (py > 0, (pz, py - 1, px)), (pz > 0, (pz - 1, py, px)))
    upper = ((px < nx_dev - 1, (pz, py, px + 1)), (py < ny_dev - 1, (pz, py + 1, px)), (pz < nz_dev - 1, (pz + 1, py, px)))

    def halo_copies(w):
        out = []
        for axis, (src, dst) in enumerate(((xs, xr), (ys, yr), (zs, zr))):
            for d in range(2):
                ok_send, dev = (lower, upper)[d][axis]
                ok_recv, _ = (upper, lower)[d][axis]
                cp = pltpu.make_async_remote_copy(
                    src_ref=src.at[d], dst_ref=dst.at[w, 1 - d], send_sem=halo_send.at[w, 2 * axis + d],
                    recv_sem=halo_recv.at[w, 2 * axis + d], device_id=dev, device_id_type=MESH)
                out.append((ok_send, ok_recv, cp))
        return out

    def k_copies():
        out = []
        for axis, (src, dst) in enumerate(((kxs, kxr), (kys, kyr), (kzs, kzr))):
            cp = pltpu.make_async_remote_copy(
                src_ref=src, dst_ref=dst, send_sem=k_send.at[axis], recv_sem=k_recv.at[axis],
                device_id=upper[axis][1], device_id_type=MESH)
            out.append((upper[axis][0], lower[axis][0], cp))
        return out

    def start_all(copies):
        for ok_send, _, cp in copies:
            pl.when(ok_send)(cp.start)

    def wait_all(copies):
        for ok_send, ok_recv, cp in copies:
            pl.when(ok_send)(cp.wait_send)
            pl.when(ok_recv)(cp.wait_recv)

    def send_dot(kind, c, acc):
        acc = jnp.sum(acc, axis=0)
        dots[kind, c, me] = jnp.sum(acc, axis=0, keepdims=True)
        each_other(lambda dev: pltpu.make_async_remote_copy(
            src_ref=dots.at[kind, c, me], dst_ref=dots.at[kind, c, me], send_sem=dot_send.at[kind, c],
            recv_sem=dot_recv.at[kind, c], device_id=dev, device_id_type=MESH).start())

    def wait_dot(kind, c):
        rows = dots.at[kind, c, pl.ds(0, n_dev - 1)]
        cp = pltpu.make_async_remote_copy(
            src_ref=rows, dst_ref=rows, send_sem=dot_send.at[kind, c], recv_sem=dot_recv.at[kind, c],
            device_id=(pz, py, px), device_id_type=MESH)
        cp.wait_recv()
        cp.wait_send()
        terms = [dots[kind, c, d] for d in range(n_dev)]
        while len(terms) > 1:
            terms = [terms[i] + terms[i + 1] for i in range(0, len(terms), 2)]
        total = jnp.sum(terms[0], axis=1, keepdims=True)
        return jnp.broadcast_to(total, (1, 128))

    def phase_a(c, beta):
        if beta is not None:
            beta = jnp.broadcast_to(beta, (8, 128))

        def new_p(*idx):
            if beta is not None:
                p[idx] = r[idx] + beta * p[idx]

        def head(yi):
            new_p(c, 0, yi + 1, zsl)
            new_p(c, 1, yi + 1, zsl)
            fx[yi] = kx[c, 0, yi] * (p[c, 0, yi + 1, zsl] - p[c, 1, yi + 1, zsl])
        unrolled(YI, head)

        def plane(xi, acc):
            new_p(c, xi + 1, ysl, 0)
            new_p(c, xi + 1, ysl, ZI + 1)
            new_p(c, xi + 1, 0, zsl)
            new_p(c, xi + 1, YI + 1, zsl)
            pc = p[c, xi + 1, 1, zsl]
            fy_lo = ky[c, xi, 0] * (p[c, xi + 1, 0, zsl] - pc)

            def line(yi, carry):
                acc, pc, fy_lo = carry
                new_p(c, xi + 2, yi + 1, zsl)
                py_hi = p[c, xi + 1, yi + 2, zsl]
                fx_lo = fx[yi]
                fx_hi = kx[c, xi + 1, yi] * (pc - p[c, xi + 2, yi + 1, zsl])
                fx[yi] = fx_hi
                fy_hi = ky[c, xi, yi + 1] * (pc - py_hi)
                fz = kz[c, xi, yi] * (p[c, xi + 1, yi + 1, :ZI + 1] - p[c, xi + 1, yi + 1, 1:])
                out = s[c, xi, yi] * pc + (fx_hi - fx_lo) + (fy_hi - fy_lo) + (fz[1:] - fz[:-1])
                q[c, xi, yi] = out
                return acc + pc * out, py_hi, fy_hi
            return lax.fori_loop(0, YI, line, (acc, pc, fy_lo), unroll=True)[0]
        return lax.fori_loop(0, XI, plane, jnp.zeros((ZI, 8, 128), jnp.float32))

    def phase_b(c, alpha):
        if alpha is not None:
            alpha = jnp.broadcast_to(alpha, (8, 128))

        def plane(xi, acc):
            def line(yi, acc):
                step = q[c, xi, yi] if alpha is None else alpha * q[c, xi, yi]
                v = r[c, xi + 1, yi + 1, zsl] - step
                r[c, xi + 1, yi + 1, zsl] = v
                return acc + v * v
            return lax.fori_loop(0, YI, line, acc, unroll=True)
        return lax.fori_loop(0, XI, plane, jnp.zeros((ZI, 8, 128), jnp.float32))

    def phase_x(c, alpha):
        alpha = jnp.broadcast_to(alpha, (8, 128))

        def plane(xi, _):
            x[c, xi] = x[c, xi] + alpha * p[c, xi + 1, ysl, zsl]
            return 0
        lax.fori_loop(0, XI, plane, 0)

    def both(fn):
        def system(c, _):
            fn(c)
            return 0
        lax.fori_loop(0, 2, system, 0)

    def put_x(c, xi, yi, zi, v):
        p[c, xi + 1, yi + 1, zi + 1] = v
        x[c, xi, yi, zi] = v
    relayout(0, put_x)
    both(lambda c: pack_field(p, c))
    start_all(halo_copies(1))

    def put_to(ref, ox, oy, oz):
        def put(c, xi, yi, zi, v):
            ref[c, xi + ox, yi + oy, zi + oz] = v
        return put
    relayout(1, put_to(kx, 1, 0, 0))
    relayout(2, put_to(ky, 0, 1, 0))
    relayout(3, put_to(kz, 0, 0, 1))

    def pack_k(c):
        def put(ref):
            def put_(v):
                ref[c] = v
            return put_
        pack_x(lambda yi: kx[c, XI, yi], ZB, put(kxs))
        pack_z(lambda xi: kz[c, xi, :, ZI], ZB - 1, put(kzs))
        kys[c] = ky[c, :, YI, :, YB - 1:YB, :]
    both(pack_k)
    start_all(k_copies())
    relayout(4, put_to(s, 0, 0, 0))
    relayout(5, put_to(r, 1, 1, 1))
    wait_all(halo_copies(1))
    both(lambda c: ghost_field(p, c, 1))
    wait_all(k_copies())

    def ghost_k(c):
        def edge(cond, v):
            return jnp.where(cond, 0.0, v)
        for yi in range(YI):
            v = kx[c, XI, yi]
            kx[c, 0, yi] = ghost_x(v, kxr[c], yi, True)
            kx[c, XI, yi] = edge(jnp.logical_and(lane_x == XB - 1, px == nx_dev - 1), v)
        for xi in range(XI):
            v = kz[c, xi, :, ZI]
            kz[c, xi, :, 0] = ghost_z(v, kzr[c], xi, True)
            kz[c, xi, :, ZI] = edge(jnp.logical_and(lane_z == ZB - 1, pz == nz_dev - 1), v)
        v = ky[c, :, YI]
        ky[c, :, 0] = ghost_y(v, kyr[c], True)
        ky[c, :, YI] = edge(jnp.logical_and(sub == YB - 1, py == ny_dev - 1), v)
    both(ghost_k)

    for c in range(2):
        phase_a(c, None)
        send_dot(1, c, phase_b(c, None))
    both(lambda c: pack_field(r, c))
    start_all(halo_copies(0))
    rho[...] = jnp.ones(rho.shape, jnp.float32)
    hist[...] = jnp.zeros(hist.shape, jnp.float32)

    def new_rho(c, k):
        total = wait_dot(1, c)
        ratio = total / rho[c]
        rho[c] = total
        hist[c] = jnp.where(row_lane == k, total, hist[c])
        return ratio

    def iteration(k, _):
        wait_all(halo_copies(0))
        both(lambda c: ghost_field(r, c, 0))
        for c in range(2):
            beta = new_rho(c, k)
            beta = jnp.where(k == 0, 0.0, beta)
            send_dot(0, c, phase_a(c, beta))
        alphas = []
        for c in range(2):
            alpha = rho[c] / wait_dot(0, c)
            alphas.append(alpha)
            send_dot(1, c, phase_b(c, alpha))

        @pl.when(k < ITERS - 1)
        def _():
            both(lambda c: pack_field(r, c))
            start_all(halo_copies(0))
        for c in range(2):
            phase_x(c, alphas[c])
        return 0
    lax.fori_loop(0, ITERS, iteration, 0)

    def system_out(c, _):
        def plane(xi, _):
            def gather(zi):
                def line(yi):
                    tmp[zi, pl.ds(yi, YB, stride=YI), :] = x[c, xi, yi, zi]
                unrolled(YI, line)
            unrolled(ZI, gather)

            def put(zi):
                stage[0, c, :, xi, pl.ds(zi, ZB, stride=ZI), :] = tmp[zi].T.reshape(XB, ZB, tmp.shape[1])
            unrolled(ZI, put)
            return 0
        lax.fori_loop(0, XI, plane, 0)
        pltpu.make_async_copy(stage.at[0, c], xo_hbm.at[c], out_sem.at[c]).start()
        return 0
    lax.fori_loop(0, 2, system_out, 0)
    for c in range(2):
        new_rho(c, ITERS)
        hist_ref[c:c + 1, :] = jnp.sqrt(hist[c] / cells)[:, :ITERS + 1]
    for c in range(2):
        pltpu.make_async_copy(stage.at[0, c], xo_hbm.at[c], out_sem.at[c]).wait()


def solution(mesh):
    sizes = tuple(mesh.shape[a] for a in AXES)
    n_dev = sizes[0] * sizes[1] * sizes[2]
    field_spec = P(None, 'px', 'py', 'pz')

    def local_solve(*args):
        _, nx, ny, nz = args[0].shape
        XI, YI, ZI = nx // XB, ny // YB, nz // ZB
        cells = float(nx * ny * nz * n_dev)
        f32 = jnp.float32
        rows = (XI, ZI, 1, 128)

        def vregs(*lead):
            return pltpu.VMEM(lead + (8, 128), f32)
        hbm = pl.BlockSpec(memory_space=pl.ANY)
        args = [jnp.swapaxes(a, 2, 3).reshape(2, XB, XI, nz, ny) for a in args]
        x_out, hist = pl.pallas_call(
            functools.partial(kernel, sizes, (XI, YI, ZI, cells)),
            out_shape=(jax.ShapeDtypeStruct((2, XB, XI, nz, ny), f32), jax.ShapeDtypeStruct((2, ITERS + 1), f32)),
            in_specs=[hbm] * 6,
            out_specs=(hbm, pl.BlockSpec(memory_space=pltpu.VMEM)),
            scratch_shapes=[
                pltpu.VMEM((6, 2, XB, XI, nz, ny), f32),
                vregs(2, XI + 2, YI + 2, ZI + 2), vregs(2, XI + 2, YI + 2, ZI + 2),
                vregs(2, XI, YI, ZI), vregs(2, XI, YI, ZI), vregs(2, XI, YI, ZI),
                vregs(2, XI + 1, YI, ZI), vregs(2, XI, YI + 1, ZI), vregs(2, XI, YI, ZI + 1),
                vregs(YI, ZI), pltpu.VMEM((ZI, ny, 128), f32),
                vregs(2, 2, ZI), vregs(2, 2, 2, ZI), pltpu.VMEM((2, 2) + rows, f32), pltpu.VMEM((2, 2, 2) + rows, f32),
                vregs(2, 2, YI), vregs(2, 2, 2, YI),
                vregs(2, ZI), vregs(2, ZI), pltpu.VMEM((2,) + rows, f32), pltpu.VMEM((2,) + rows, f32),
                vregs(2, YI), vregs(2, YI),
                pltpu.VMEM((2, 2, n_dev, 1, 128), f32), pltpu.VMEM((2, 1, 128), f32), pltpu.VMEM((2, 1, 128), f32),
                pltpu.SemaphoreType.DMA((6, 2)), pltpu.SemaphoreType.DMA((2,)),
                pltpu.SemaphoreType.DMA((2, 2)), pltpu.SemaphoreType.DMA((2, 2)),
                pltpu.SemaphoreType.DMA((2, 6)), pltpu.SemaphoreType.DMA((2, 6)),
                pltpu.SemaphoreType.DMA((3,)), pltpu.SemaphoreType.DMA((3,)),
            ],
            compiler_params=pltpu.CompilerParams(collective_id=0, has_side_effects=True, vmem_limit_bytes=67043328),
            name='cg',
        )(*args)
        return jnp.swapaxes(x_out.reshape(2, nx, nz, ny), 2, 3), hist

    return jax.shard_map(local_solve, mesh=mesh, in_specs=(field_spec,) * 6, out_specs=(field_spec, P(None, None)), check_vma=False)
```

time: 3320 us -> 281 us (0.08)
  blocking collectives: 1750 us -> 0 us
  other arithmetic: 825 us -> 0 us
  local copies, waits for them, and re-layouts: 473 us -> 4.86 us
  Pallas kernels: 0 us -> 275 us
  starting transfers between devices: 254 us -> 0 us
    psum x41 -> x0, blocking collectives: 1750 us -> none  [global_dot(): return lax.psum(jnp.sum(left_vec * right_vec, axis=(1, 2, 3)), ALL_AXES)]
    mul x61 -> x0, other arithmetic: 355 us -> none  [apply_local(): cond_ext[axis_pos]]
    slice x106 -> x0, local copies, waits for them, and re-layouts: 331 us -> none  [the longest x83 265 us: neighbour_planes(): first_plane = lax.slice_in_dim(field, 0, 1, axis=axis_dim)]
    reduce_sum x41 -> x0, other arithmetic: 309 us -> none  [global_dot(): return lax.psum(jnp.sum(left_vec * right_vec, axis=(1, 2, 3)), ALL_AXES)]
    pallas_call x0 -> x1, Pallas kernels: none -> 275 us  [local_solve(): pl.pallas_call(functools.partial(kernel, sizes, (XI, YI, ZI, cells)), out...]
    ppermute x129 -> x0, starting transfers between devices: 254 us -> none  [the longest x63 158 us: neighbour_planes(): from_below = lax.ppermute(last_plane, axis_name, up_pairs(axis_size))]
    ppermute x43 -> x0, local copies, waits for them, and re-layouts: 120 us -> none  [the longest x21 58.9 us: neighbour_planes(): from_below = lax.ppermute(last_plane, axis_name, up_pairs(axis_size))]
    add x20 -> x0, other arithmetic: 113 us -> none  [cg_step(): direction = res_cur + beta_coef[:, None, None, None] * direction]
  transfers between devices with their start and end apart: 129 -> 0, of which waited for: 0 -> 0; matrix products, arithmetic and copies ran while one was open for 16% -> 0% of each run, Pallas kernels for 0% -> 0%
where the time goes in v1:
time: 281 us
  Pallas kernels  275 us (98%)
  local copies, waits for them, and re-layouts  4.86 us (2%)
    pallas_call x1, Pallas kernels, local_solve(): pl.pallas_call(functools.partial(kernel, sizes, (XI, YI, ZI, cells)), out...  275 us

profile of v1, /device:TPU:0, one launch (start us, length us, event | category | flops | bytes accessed | tf_op | source)
XLA Modules:
  0.0 280.6 jit_solution(15091525175267955237)
XLA Ops:
  0.6 275.1 %cg.1 = (f32[2,16,5,48,80]{4,3,2,1,0:T(8,128)}, f32[2,21]{1,0:T(2,128)}) custom-call(f32[2,16,5,48,80]{4,3,2,1,0:T(8,128)} %bitcast.21, f32[2,16,5,48,80]{4,3,2,1,0:T(8,128)} %bitcast.22, f32[2,16,5,48,80]{4,3,2,1,0:T(8,128)} %bitcast.23, f32[2,16,5,48,80]{4,3,2,1,0:T(8,128)} %bitcast.24, f32[2,16,5,48,80]{4,3,2,1,0:T(8,128)} %bitcast.25, ...), custom_call_target="tpu_custom_call" | custom-call | tf_op jit(solution)/shard_map/cg/pallas_call | solution.py:374
  275.8 0.0 copy-start
  275.8 4.3 %copy.10 = f32[2,80,80,48]{2,3,1,0:T(8,128)} copy(f32[2,80,80,48]{2,3,1,0:T(8,128)} %bitcast.27) | data formatting | bytes 4915200
  280.1 0.0 copy-done
  280.1 0.6 copy.11
Async XLA Ops:
  275.8 4.3 %copy-start = (f32[2,21]{1,0:T(2,128)S(1)}, f32[2,21]{1,0:T(2,128)}, u32[]{:S(2)}) copy-start(f32[2,21]{1,0:T(2,128)} %get-tuple-element.9) | copy-start | bytes 508

commit v2 on v1

--- a/solution.py
+++ b/solution.py
@@ -109,17 +109,18 @@
         moved = pltpu.roll(v, 1 if low else YB - 1, v.ndim - 2)
         return jnp.where(sub == dst, jnp.broadcast_to(rows, v.shape), moved)
 
-    def pack_field(f, c):
+    def pack_field(f, c, o):
         def put(ref, d):
             def put_(v):
                 ref[d, c] = v
             return put_
-        pack_x(lambda yi: f[c, 1, yi + 1, zsl], 0, put(xs, 0))
-        pack_x(lambda yi: f[c, XI, yi + 1, zsl], ZB, put(xs, 1))
-        pack_z(lambda xi: f[c, xi + 1, ysl, 1], 0, put(zs, 0))
-        pack_z(lambda xi: f[c, xi + 1, ysl, ZI], ZB - 1, put(zs, 1))
-        ys[0, c] = f[c, xsl, 1, zsl, 0:1, :]
-        ys[1, c] = f[c, xsl, YI, zsl, YB - 1:YB, :]
+        xa, ya, za = slice(o, o + XI), slice(o, o + YI), slice(o, o + ZI)
+        pack_x(lambda yi: f[c, o, yi + o, za], 0, put(xs, 0))
+        pack_x(lambda yi: f[c, XI - 1 + o, yi + o, za], ZB, put(xs, 1))
+        pack_z(lambda xi: f[c, xi + o, ya, o], 0, put(zs, 0))
+        pack_z(lambda xi: f[c, xi + o, ya, ZI - 1 + o], ZB - 1, put(zs, 1))
+        ys[0, c] = f[c, xa, o, za, 0:1, :]
+        ys[1, c] = f[c, xa, YI - 1 + o, za, YB - 1:YB, :]
 
     def ghost_field(f, c, w):
         for yi in range(YI):
@@ -252,7 +253,7 @@
         p[c, xi + 1, yi + 1, zi + 1] = v
         x[c, xi, yi, zi] = v
     relayout(0, put_x)
-    both(lambda c: pack_field(p, c))
+    both(lambda c: pack_field(p, c, 1))
     start_all(halo_copies(1))
 
     def put_to(ref, ox, oy, oz):
@@ -298,10 +299,12 @@
     for c in range(2):
         phase_a(c, None)
         send_dot(1, c, phase_b(c, None))
-    both(lambda c: pack_field(r, c))
+    both(lambda c: pack_field(r, c, 1))
     start_all(halo_copies(0))
     rho[...] = jnp.ones(rho.shape, jnp.float32)
     hist[...] = jnp.zeros(hist.shape, jnp.float32)
+    wait_all(halo_copies(0))
+    both(lambda c: ghost_field(r, c, 0))
 
     def new_rho(c, k):
         total = wait_dot(1, c)
@@ -311,48 +314,67 @@
         return ratio
 
     def iteration(k, _):
-        wait_all(halo_copies(0))
-        both(lambda c: ghost_field(r, c, 0))
+        slot = 2 + lax.rem(k, 2)
         for c in range(2):
             beta = new_rho(c, k)
             beta = jnp.where(k == 0, 0.0, beta)
             send_dot(0, c, phase_a(c, beta))
+
+        @pl.when(k < ITERS - 1)
+        def _():
+            both(lambda c: pack_field(q, c, 0))
+            start_all(halo_copies(slot))
         alphas = []
         for c in range(2):
             alpha = rho[c] / wait_dot(0, c)
             alphas.append(alpha)
             send_dot(1, c, phase_b(c, alpha))
+        for c in range(2):
+            phase_x(c, alphas[c])
 
         @pl.when(k < ITERS - 1)
         def _():
-            both(lambda c: pack_field(r, c))
-            start_all(halo_copies(0))
-        for c in range(2):
-            phase_x(c, alphas[c])
+            wait_all(halo_copies(slot))
+            for ref in (xr, yr, zr):
+                for d in range(2):
+                    for c in range(2):
+                        ref[0, d, c] = ref[0, d, c] - alphas[c] * ref[slot, d, c]
+            both(lambda c: ghost_field(r, c, 0))
         return 0
     lax.fori_loop(0, ITERS, iteration, 0)
 
-    def system_out(c, _):
+    for c in range(2):
+        pltpu.make_async_copy(x.at[c], xo_hbm.at[c], out_sem.at[c]).start()
+    for c in range(2):
+        new_rho(c, ITERS)
+        hist_ref[c:c + 1, :] = jnp.sqrt(hist[c] / cells)[:, :ITERS + 1]
+    for c in range(2):
+        pltpu.make_async_copy(x.at[c], xo_hbm.at[c], out_sem.at[c]).wait()
+
+
+def cell_order(dims, x_hbm, o_hbm, x, stage, tmp, in_sem, out_sem):
+    XI, YI, ZI = dims
+    for c in range(2):
+        pltpu.make_async_copy(x_hbm.at[c], x.at[c], in_sem.at[c]).start()
+
+    def out_copy(c, xi):
+        return pltpu.make_async_copy(stage.at[c, :, xi], o_hbm.at[c, :, xi], out_sem.at[c, xi])
+
+    for c in range(2):
+        pltpu.make_async_copy(x_hbm.at[c], x.at[c], in_sem.at[c]).wait()
+
         def plane(xi, _):
-            def gather(zi):
-                def line(yi):
+            for zi in range(ZI):
+                for yi in range(YI):
                     tmp[zi, pl.ds(yi, YB, stride=YI), :] = x[c, xi, yi, zi]
-                unrolled(YI, line)
-            unrolled(ZI, gather)
-
-            def put(zi):
-                stage[0, c, :, xi, pl.ds(zi, ZB, stride=ZI), :] = tmp[zi].T.reshape(XB, ZB, tmp.shape[1])
-            unrolled(ZI, put)
+            for zi in range(ZI):
+                stage[c, :, xi, pl.ds(zi, ZB, stride=ZI), :] = tmp[zi].T.reshape(XB, ZB, tmp.shape[1])
+            out_copy(c, xi).start()
             return 0
         lax.fori_loop(0, XI, plane, 0)
-        pltpu.make_async_copy(stage.at[0, c], xo_hbm.at[c], out_sem.at[c]).start()
-        return 0
-    lax.fori_loop(0, 2, system_out, 0)
-    for c in range(2):
-        new_rho(c, ITERS)
-        hist_ref[c:c + 1, :] = jnp.sqrt(hist[c] / cells)[:, :ITERS + 1]
-    for c in range(2):
-        pltpu.make_async_copy(stage.at[0, c], xo_hbm.at[c], out_sem.at[c]).wait()
+    for c in range(2):
+        for xi in range(XI):
+            out_copy(c, xi).wait()
 
 
 def solution(mesh):
@@ -373,7 +395,7 @@
         args = [jnp.swapaxes(a, 2, 3).reshape(2, XB, XI, nz, ny) for a in args]
         x_out, hist = pl.pallas_call(
             functools.partial(kernel, sizes, (XI, YI, ZI, cells)),
-            out_shape=(jax.ShapeDtypeStruct((2, XB, XI, nz, ny), f32), jax.ShapeDtypeStruct((2, ITERS + 1), f32)),
+            out_shape=(jax.ShapeDtypeStruct((2, XI, YI, ZI, 8, 128), f32), jax.ShapeDtypeStruct((2, ITERS + 1), f32)),
             in_specs=[hbm] * 6,
             out_specs=(hbm, pl.BlockSpec(memory_space=pltpu.VMEM)),
             scratch_shapes=[
@@ -382,19 +404,30 @@
                 vregs(2, XI, YI, ZI), vregs(2, XI, YI, ZI), vregs(2, XI, YI, ZI),
                 vregs(2, XI + 1, YI, ZI), vregs(2, XI, YI + 1, ZI), vregs(2, XI, YI, ZI + 1),
                 vregs(YI, ZI), pltpu.VMEM((ZI, ny, 128), f32),
-                vregs(2, 2, ZI), vregs(2, 2, 2, ZI), pltpu.VMEM((2, 2) + rows, f32), pltpu.VMEM((2, 2, 2) + rows, f32),
-                vregs(2, 2, YI), vregs(2, 2, 2, YI),
+                vregs(2, 2, ZI), vregs(4, 2, 2, ZI), pltpu.VMEM((2, 2) + rows, f32), pltpu.VMEM((4, 2, 2) + rows, f32),
+                vregs(2, 2, YI), vregs(4, 2, 2, YI),
                 vregs(2, ZI), vregs(2, ZI), pltpu.VMEM((2,) + rows, f32), pltpu.VMEM((2,) + rows, f32),
                 vregs(2, YI), vregs(2, YI),
                 pltpu.VMEM((2, 2, n_dev, 1, 128), f32), pltpu.VMEM((2, 1, 128), f32), pltpu.VMEM((2, 1, 128), f32),
                 pltpu.SemaphoreType.DMA((6, 2)), pltpu.SemaphoreType.DMA((2,)),
                 pltpu.SemaphoreType.DMA((2, 2)), pltpu.SemaphoreType.DMA((2, 2)),
-                pltpu.SemaphoreType.DMA((2, 6)), pltpu.SemaphoreType.DMA((2, 6)),
+                pltpu.SemaphoreType.DMA((4, 6)), pltpu.SemaphoreType.DMA((4, 6)),
                 pltpu.SemaphoreType.DMA((3,)), pltpu.SemaphoreType.DMA((3,)),
             ],
             compiler_params=pltpu.CompilerParams(collective_id=0, has_side_effects=True, vmem_limit_bytes=67043328),
             name='cg',
         )(*args)
+        x_out = pl.pallas_call(
+            functools.partial(cell_order, (XI, YI, ZI)),
+            out_shape=jax.ShapeDtypeStruct((2, XB, XI, nz, ny), f32),
+            in_specs=[hbm], out_specs=hbm,
+            scratch_shapes=[
+                vregs(2, XI, YI, ZI), pltpu.VMEM((2, XB, XI, nz, ny), f32), pltpu.VMEM((ZI, ny, 128), f32),
+                pltpu.SemaphoreType.DMA((2,)), pltpu.SemaphoreType.DMA((2, XI)),
+            ],
+            compiler_params=pltpu.CompilerParams(vmem_limit_bytes=67043328),
+            name='cell_order',
+        )(x_out)
         return jnp.swapaxes(x_out.reshape(2, nx, nz, ny), 2, 3), hist
 
     return jax.shard_map(local_solve, mesh=mesh, in_specs=(field_spec,) * 6, out_specs=(field_spec, P(None, None)), check_vma=False)

time: 281 us -> 250 us (0.89)
  Pallas kernels: 275 us -> 248 us
  local copies, waits for them, and re-layouts: 4.86 us -> 1.22 us
    pallas_call x1, Pallas kernels: 275 us -> 244 us  [local_solve(): pl.pallas_call(functools.partial(kernel, sizes, (XI, YI, ZI, cells)), out...]
    pallas_call x0 -> x1, Pallas kernels: none -> 3.96 us  [local_solve(): pl.pallas_call(functools.partial(cell_order, (XI, YI, ZI)), out_shape=jax...]
    unnamed x4 -> x1, local copies, waits for them, and re-layouts: 4.86 us -> 1.22 us
where the time goes in v2:
time: 250 us
  Pallas kernels  248 us (99%)
    pallas_call x1, Pallas kernels, local_solve(): pl.pallas_call(functools.partial(kernel, sizes, (XI, YI, ZI, cells)), out...  244 us

profile of v2, /device:TPU:0, one launch (start us, length us, event | category | flops | bytes accessed | tf_op | source)
XLA Modules:
  0.0 249.6 jit_solution(5174744729094598143)
XLA Ops:
  0.6 243.7 %cg.1 = (f32[2,5,10,6,8,128]{5,4,3,2,1,0:T(8,128)}, f32[2,21]{1,0:T(2,128)}) custom-call(f32[2,16,5,48,80]{4,3,2,1,0:T(8,128)} %bitcast.21, f32[2,16,5,48,80]{4,3,2,1,0:T(8,128)} %bitcast.22, f32[2,16,5,48,80]{4,3,2,1,0:T(8,128)} %bitcast.23, f32[2,16,5,48,80]{4,3,2,1,0:T(8,128)} %bitcast.24, f32[2,16,5,48,80]{4,3,2,1,0:T(8,128)} %bitcast.25, ...), custom_call_target="tpu_custom_call" | custom-call | tf_op jit(solution)/shard_map/cg/pallas_call | solution.py:396
  244.4 4.0 %cell_order.1 = f32[2,16,5,48,80]{4,3,2,1,0:T(8,128)} custom-call(f32[2,5,10,6,8,128]{5,4,3,2,1,0:T(8,128)} %get-tuple-element.4.x_hbm), custom_call_target="tpu_custom_call" | custom-call | tf_op jit(solution)/shard_map/cell_order/pallas_call | solution.py:420
  248.4 1.2 copy.9

commit v3 on v2

--- a/solution.py
+++ b/solution.py
@@ -41,16 +41,21 @@
     for ref in (xr, yr, zr, kxr, kyr, kzr):
         ref[...] = jnp.zeros(ref.shape, ref.dtype)
 
-    def target(off):
-        t = lax.rem(me + off, n_dev)
-        rest = lax.rem(t, ny_dev * nx_dev)
-        return (lax.div(t, ny_dev * nx_dev), lax.div(rest, nx_dev), lax.rem(rest, nx_dev))
+    def far_first(pos, size, n):
+        high = lax.div(2 * pos, size)
+        return high * n + (1 - high) * (size - 1 - n)
 
     def each_other(fn):
-        def step(i, _):
-            fn(target(i))
+        def step(n, _):
+            dev = (far_first(pz, nz_dev, lax.div(n, ny_dev * nx_dev)),
+                   far_first(py, ny_dev, lax.rem(lax.div(n, nx_dev), ny_dev)),
+                   far_first(px, nx_dev, lax.rem(n, nx_dev)))
+
+            @pl.when((dev[0] * ny_dev + dev[1]) * nx_dev + dev[2] != me)
+            def _():
+                fn(dev)
             return 0
-        lax.fori_loop(1, n_dev, step, 0, unroll=True)
+        lax.fori_loop(0, n_dev, step, 0, unroll=True)
 
     barrier = pltpu.get_barrier_semaphore()
     each_other(lambda dev: pl.semaphore_signal(barrier, inc=1, device_id=dev, device_id_type=MESH))
@@ -64,6 +69,7 @@
 
     ysl, zsl = slice(1, YI + 1), slice(1, ZI + 1)
     xsl = slice(1, XI + 1)
+    ytail = slice(min(YI, ZB) + 1, YI + 1)
 
     def relayout(a, stores):
         def system(c, _):
@@ -85,12 +91,19 @@
             acc = jnp.where(lane_x == j, pltpu.roll(get(j), (shift + ZB * j) % 128, 2), acc)
         put(acc)
 
+    ycut = min(YI, ZB)
+
     def pack_z(get, src_zb, put):
-        acc = pltpu.roll(get(0), (-src_zb) % 128, 2) if src_zb else get(0)
-        for j in range(1, XI):
-            v = get(j)
-            acc = jnp.where(lane_z == j, pltpu.roll(v, (j - src_zb) % 128, 2) if j != src_zb else v, acc)
-        put(acc)
+        def merge(count, part):
+            acc = None
+            for j in range(count):
+                v = part(j)
+                v = pltpu.roll(v, (j - src_zb) % 128, 2) if j != src_zb else v
+                acc = v if acc is None else jnp.where(lane_z == j, v, acc)
+            return acc
+        put(slice(0, XI), merge(ycut, lambda yi: get(slice(0, XI), yi)))
+        if YI > ycut:
+            put(slice(XI, XI + YI - ycut), merge(XI, lambda xi: get(xi, slice(ycut, YI))))
 
     def ghost_x(v, packed, j, low):
         dst = 0 if low else XB - 1
@@ -111,14 +124,17 @@
 
     def pack_field(f, c, o):
         def put(ref, d):
-            def put_(v):
-                ref[d, c] = v
+            def put_(*v):
+                ref[(d, c) + v[:-1]] = v[-1]
             return put_
-        xa, ya, za = slice(o, o + XI), slice(o, o + YI), slice(o, o + ZI)
+        xa, za = slice(o, o + XI), slice(o, o + ZI)
+
+        def line(i):
+            return slice(i.start + o, i.stop + o) if isinstance(i, slice) else i + o
         pack_x(lambda yi: f[c, o, yi + o, za], 0, put(xs, 0))
         pack_x(lambda yi: f[c, XI - 1 + o, yi + o, za], ZB, put(xs, 1))
-        pack_z(lambda xi: f[c, xi + o, ya, o], 0, put(zs, 0))
-        pack_z(lambda xi: f[c, xi + o, ya, ZI - 1 + o], ZB - 1, put(zs, 1))
+        pack_z(lambda xi, yi: f[c, line(xi), line(yi), o], 0, put(zs, 0))
+        pack_z(lambda xi, yi: f[c, line(xi), line(yi), ZI - 1 + o], ZB - 1, put(zs, 1))
         ys[0, c] = f[c, xa, o, za, 0:1, :]
         ys[1, c] = f[c, xa, YI - 1 + o, za, YB - 1:YB, :]
 
@@ -126,9 +142,13 @@
         for yi in range(YI):
             f[c, 0, yi + 1, zsl] = ghost_x(f[c, XI, yi + 1, zsl], xr[w, 0, c], yi, True)
             f[c, XI + 1, yi + 1, zsl] = ghost_x(f[c, 1, yi + 1, zsl], xr[w, 1, c], yi, False)
-        for xi in range(XI):
-            f[c, xi + 1, ysl, 0] = ghost_z(f[c, xi + 1, ysl, ZI], zr[w, 0, c], xi, True)
-            f[c, xi + 1, ysl, ZI + 1] = ghost_z(f[c, xi + 1, ysl, 1], zr[w, 1, c], xi, False)
+        for yi in range(ycut):
+            f[c, xsl, yi + 1, 0] = ghost_z(f[c, xsl, yi + 1, ZI], zr[w, 0, c, :XI], yi, True)
+            f[c, xsl, yi + 1, ZI + 1] = ghost_z(f[c, xsl, yi + 1, 1], zr[w, 1, c, :XI], yi, False)
+        if YI > ycut:
+            for xi in range(XI):
+                f[c, xi + 1, ytail, 0] = ghost_z(f[c, xi + 1, ytail, ZI], zr[w, 0, c, XI:], xi, True)
+                f[c, xi + 1, ytail, ZI + 1] = ghost_z(f[c, xi + 1, ytail, 1], zr[w, 1, c, XI:], xi, False)
         f[c, xsl, 0, zsl] = ghost_y(f[c, xsl, YI, zsl], yr[w, 0, c], True)
         f[c, xsl, YI + 1, zsl] = ghost_y(f[c, xsl, 1, zsl], yr[w, 1, c], False)
 
@@ -266,11 +286,11 @@
 
     def pack_k(c):
         def put(ref):
-            def put_(v):
-                ref[c] = v
+            def put_(*v):
+                ref[(c,) + v[:-1]] = v[-1]
             return put_
         pack_x(lambda yi: kx[c, XI, yi], ZB, put(kxs))
-        pack_z(lambda xi: kz[c, xi, :, ZI], ZB - 1, put(kzs))
+        pack_z(lambda xi, yi: kz[c, xi, yi, ZI], ZB - 1, put(kzs))
         kys[c] = ky[c, :, YI, :, YB - 1:YB, :]
     both(pack_k)
     start_all(k_copies())
@@ -287,10 +307,12 @@
             v = kx[c, XI, yi]
             kx[c, 0, yi] = ghost_x(v, kxr[c], yi, True)
             kx[c, XI, yi] = edge(jnp.logical_and(lane_x == XB - 1, px == nx_dev - 1), v)
-        for xi in range(XI):
-            v = kz[c, xi, :, ZI]
-            kz[c, xi, :, 0] = ghost_z(v, kzr[c], xi, True)
-            kz[c, xi, :, ZI] = edge(jnp.logical_and(lane_z == ZB - 1, pz == nz_dev - 1), v)
+        for yi in range(ycut):
+            kz[c, :, yi, 0] = ghost_z(kz[c, :, yi, ZI], kzr[c, :XI], yi, True)
+        if YI > ycut:
+            for xi in range(XI):
+                kz[c, xi, ycut:, 0] = ghost_z(kz[c, xi, ycut:, ZI], kzr[c, XI:], xi, True)
+        kz[c, :, :, ZI] = edge(jnp.logical_and(lane_z == ZB - 1, pz == nz_dev - 1), kz[c, :, :, ZI])
         v = ky[c, :, YI]
         ky[c, :, 0] = ghost_y(v, kyr[c], True)
         ky[c, :, YI] = edge(jnp.logical_and(sub == YB - 1, py == ny_dev - 1), v)
@@ -352,18 +374,22 @@
         pltpu.make_async_copy(x.at[c], xo_hbm.at[c], out_sem.at[c]).wait()
 
 
-def cell_order(dims, x_hbm, o_hbm, x, stage, tmp, in_sem, out_sem):
+def cell_order(dims, x_hbm, hist_in, o_hbm, hist_out, x, stage, tmp, in_sem, out_sem):
     XI, YI, ZI = dims
-    for c in range(2):
-        pltpu.make_async_copy(x_hbm.at[c], x.at[c], in_sem.at[c]).start()
+
+    def in_copy(c, xi):
+        return pltpu.make_async_copy(x_hbm.at[c, xi], x.at[c, xi], in_sem.at[c, xi])
 
     def out_copy(c, xi):
         return pltpu.make_async_copy(stage.at[c, :, xi], o_hbm.at[c, :, xi], out_sem.at[c, xi])
 
     for c in range(2):
-        pltpu.make_async_copy(x_hbm.at[c], x.at[c], in_sem.at[c]).wait()
-
+        for xi in range(XI):
+            in_copy(c, xi).start()
+    hist_out[...] = hist_in[...]
+    for c in range(2):
         def plane(xi, _):
+            in_copy(c, xi).wait()
             for zi in range(ZI):
                 for yi in range(YI):
                     tmp[zi, pl.ds(yi, YB, stride=YI), :] = x[c, xi, yi, zi]
@@ -388,6 +414,7 @@
         cells = float(nx * ny * nz * n_dev)
         f32 = jnp.float32
         rows = (XI, ZI, 1, 128)
+        mz = XI + max(0, YI - ZB)
 
         def vregs(*lead):
             return pltpu.VMEM(lead + (8, 128), f32)
@@ -405,9 +432,9 @@
                 vregs(2, XI + 1, YI, ZI), vregs(2, XI, YI + 1, ZI), vregs(2, XI, YI, ZI + 1),
                 vregs(YI, ZI), pltpu.VMEM((ZI, ny, 128), f32),
                 vregs(2, 2, ZI), vregs(4, 2, 2, ZI), pltpu.VMEM((2, 2) + rows, f32), pltpu.VMEM((4, 2, 2) + rows, f32),
-                vregs(2, 2, YI), vregs(4, 2, 2, YI),
+                vregs(2, 2, mz), vregs(4, 2, 2, mz),
                 vregs(2, ZI), vregs(2, ZI), pltpu.VMEM((2,) + rows, f32), pltpu.VMEM((2,) + rows, f32),
-                vregs(2, YI), vregs(2, YI),
+                vregs(2, mz), vregs(2, mz),
                 pltpu.VMEM((2, 2, n_dev, 1, 128), f32), pltpu.VMEM((2, 1, 128), f32), pltpu.VMEM((2, 1, 128), f32),
                 pltpu.SemaphoreType.DMA((6, 2)), pltpu.SemaphoreType.DMA((2,)),
                 pltpu.SemaphoreType.DMA((2, 2)), pltpu.SemaphoreType.DMA((2, 2)),
@@ -417,17 +444,18 @@
             compiler_params=pltpu.CompilerParams(collective_id=0, has_side_effects=True, vmem_limit_bytes=67043328),
             name='cg',
         )(*args)
-        x_out = pl.pallas_call(
+        small = pl.BlockSpec(memory_space=pltpu.VMEM)
+        x_out, hist = pl.pallas_call(
             functools.partial(cell_order, (XI, YI, ZI)),
-            out_shape=jax.ShapeDtypeStruct((2, XB, XI, nz, ny), f32),
-            in_specs=[hbm], out_specs=hbm,
+            out_shape=(jax.ShapeDtypeStruct((2, XB, XI, nz, ny), f32), jax.ShapeDtypeStruct(hist.shape, f32)),
+            in_specs=[hbm, small], out_specs=(hbm, small),
             scratch_shapes=[
                 vregs(2, XI, YI, ZI), pltpu.VMEM((2, XB, XI, nz, ny), f32), pltpu.VMEM((ZI, ny, 128), f32),
-                pltpu.SemaphoreType.DMA((2,)), pltpu.SemaphoreType.DMA((2, XI)),
+                pltpu.SemaphoreType.DMA((2, XI)), pltpu.SemaphoreType.DMA((2, XI)),
             ],
             compiler_params=pltpu.CompilerParams(vmem_limit_bytes=67043328),
             name='cell_order',
-        )(x_out)
+        )(x_out, hist)
         return jnp.swapaxes(x_out.reshape(2, nx, nz, ny), 2, 3), hist
 
     return jax.shard_map(local_solve, mesh=mesh, in_specs=(field_spec,) * 6, out_specs=(field_spec, P(None, None)), check_vma=False)

time: 250 us -> 237 us (0.948)
  Pallas kernels: 248 us -> 236 us
    pallas_call x1, Pallas kernels: 244 us -> 231 us  [local_solve(): pl.pallas_call(functools.partial(kernel, sizes, (XI, YI, ZI, cells)), out...]
where the time goes in v3:
time: 237 us
  Pallas kernels  236 us (100%)
    pallas_call x1, Pallas kernels, local_solve(): pl.pallas_call(functools.partial(kernel, sizes, (XI, YI, ZI, cells)), out...  231 us
    pallas_call x1, Pallas kernels, local_solve(): pl.pallas_call(functools.partial(cell_order, (XI, YI, ZI)), out_shape=(ja...  4.92 us

profile of v3, /device:TPU:0, one launch (start us, length us, event | category | flops | bytes accessed | tf_op | source)
XLA Modules:
  0.0 237.0 jit_solution(10244237133049140303)
XLA Ops:
  0.6 231.5 %cg.1 = (f32[2,5,10,6,8,128]{5,4,3,2,1,0:T(8,128)}, f32[2,21]{1,0:T(2,128)}) custom-call(f32[2,16,5,48,80]{4,3,2,1,0:T(8,128)} %bitcast.21, f32[2,16,5,48,80]{4,3,2,1,0:T(8,128)} %bitcast.22, f32[2,16,5,48,80]{4,3,2,1,0:T(8,128)} %bitcast.23, f32[2,16,5,48,80]{4,3,2,1,0:T(8,128)} %bitcast.24, f32[2,16,5,48,80]{4,3,2,1,0:T(8,128)} %bitcast.25, ...), custom_call_target="tpu_custom_call" | custom-call | tf_op jit(solution)/shard_map/cg/pallas_call | solution.py:423
  232.1 4.9 %cell_order.1 = (f32[2,16,5,48,80]{4,3,2,1,0:T(8,128)}, f32[2,21]{1,0:T(2,128)}) custom-call(f32[2,5,10,6,8,128]{5,4,3,2,1,0:T(8,128)} %get-tuple-element.6.x_hbm, f32[2,21]{1,0:T(2,128)} %get-tuple-element.7.hist_in), custom_call_target="tpu_custom_call" | custom-call | tf_op jit(solution)/shard_map/cell_order/pallas_call | solution.py:448

commit v4 on v3

--- a/solution.py
+++ b/solution.py
@@ -14,7 +14,7 @@
 
 
 def kernel(sizes, dims, s_hbm, b_hbm, x_hbm, kx_hbm, ky_hbm, kz_hbm, xo_hbm, hist_ref,
-           stage, r, p, q, x, s, kx, ky, kz, fx, tmp,
+           stage, r, p, q, x, s, kx, ky, kz, tmp,
            xs, xr, ys, yr, zs, zr, kxs, kxr, kys, kyr, kzs, kzr,
            dots, rho, hist,
            in_sem, out_sem, dot_send, dot_recv, halo_send, halo_recv, k_send, k_recv):
@@ -59,7 +59,6 @@
 
     barrier = pltpu.get_barrier_semaphore()
     each_other(lambda dev: pl.semaphore_signal(barrier, inc=1, device_id=dev, device_id_type=MESH))
-    pl.semaphore_wait(barrier, n_dev - 1)
 
     def unrolled(n, fn):
         def step(i, _):
@@ -216,7 +215,6 @@
         def head(yi):
             new_p(c, 0, yi + 1, zsl)
             new_p(c, 1, yi + 1, zsl)
-            fx[yi] = kx[c, 0, yi] * (p[c, 0, yi + 1, zsl] - p[c, 1, yi + 1, zsl])
         unrolled(YI, head)
 
         def plane(xi, acc):
@@ -224,22 +222,21 @@
             new_p(c, xi + 1, ysl, ZI + 1)
             new_p(c, xi + 1, 0, zsl)
             new_p(c, xi + 1, YI + 1, zsl)
-            pc = p[c, xi + 1, 1, zsl]
-            fy_lo = ky[c, xi, 0] * (p[c, xi + 1, 0, zsl] - pc)
 
             def line(yi, carry):
-                acc, pc, fy_lo = carry
+                acc, py_lo, pc, ky_lo = carry
                 new_p(c, xi + 2, yi + 1, zsl)
                 py_hi = p[c, xi + 1, yi + 2, zsl]
-                fx_lo = fx[yi]
-                fx_hi = kx[c, xi + 1, yi] * (pc - p[c, xi + 2, yi + 1, zsl])
-                fx[yi] = fx_hi
-                fy_hi = ky[c, xi, yi + 1] * (pc - py_hi)
-                fz = kz[c, xi, yi] * (p[c, xi + 1, yi + 1, :ZI + 1] - p[c, xi + 1, yi + 1, 1:])
-                out = s[c, xi, yi] * pc + (fx_hi - fx_lo) + (fy_hi - fy_lo) + (fz[1:] - fz[:-1])
+                ky_hi = ky[c, xi, yi + 1]
+                out = s[c, xi, yi] * pc - ky_lo * py_lo - ky_hi * py_hi
+                out = out - kx[c, xi, yi] * p[c, xi, yi + 1, zsl]
+                out = out - kz[c, xi, yi, :ZI] * p[c, xi + 1, yi + 1, :ZI]
+                out = out - kz[c, xi, yi, 1:] * p[c, xi + 1, yi + 1, 2:]
+                out = out - kx[c, xi + 1, yi] * p[c, xi + 2, yi + 1, zsl]
                 q[c, xi, yi] = out
-                return acc + pc * out, py_hi, fy_hi
-            return lax.fori_loop(0, YI, line, (acc, pc, fy_lo), unroll=True)[0]
+                return acc + pc * out, pc, py_hi, ky_hi
+            carry = (acc, p[c, xi + 1, 0, zsl], p[c, xi + 1, 1, zsl], ky[c, xi, 0])
+            return lax.fori_loop(0, YI, line, carry, unroll=True)[0]
         return lax.fori_loop(0, XI, plane, jnp.zeros((ZI, 8, 128), jnp.float32))
 
     def phase_b(c, alpha):
@@ -274,35 +271,39 @@
         x[c, xi, yi, zi] = v
     relayout(0, put_x)
     both(lambda c: pack_field(p, c, 1))
-    start_all(halo_copies(1))
 
     def put_to(ref, ox, oy, oz):
         def put(c, xi, yi, zi, v):
             ref[c, xi + ox, yi + oy, zi + oz] = v
         return put
+
+    def put_k(ref, c):
+        def put_(*v):
+            ref[(c,) + v[:-1]] = v[-1]
+        return put_
+
+    def edge(cond, v):
+        return jnp.where(cond, 0.0, v)
+    copies_x, copies_y, copies_z = k_copies()
+    relayout(3, put_to(kz, 0, 0, 1))
+    both(lambda c: pack_z(lambda xi, yi: kz[c, xi, yi, ZI], ZB - 1, put_k(kzs, c)))
+    pl.semaphore_wait(barrier, n_dev - 1)
+    start_all(halo_copies(1))
+    start_all([copies_z])
     relayout(1, put_to(kx, 1, 0, 0))
+    both(lambda c: pack_x(lambda yi: kx[c, XI, yi], ZB, put_k(kxs, c)))
+    start_all([copies_x])
     relayout(2, put_to(ky, 0, 1, 0))
-    relayout(3, put_to(kz, 0, 0, 1))
-
-    def pack_k(c):
-        def put(ref):
-            def put_(*v):
-                ref[(c,) + v[:-1]] = v[-1]
-            return put_
-        pack_x(lambda yi: kx[c, XI, yi], ZB, put(kxs))
-        pack_z(lambda xi, yi: kz[c, xi, yi, ZI], ZB - 1, put(kzs))
+    for c in range(2):
         kys[c] = ky[c, :, YI, :, YB - 1:YB, :]
-    both(pack_k)
-    start_all(k_copies())
+    start_all([copies_y])
     relayout(4, put_to(s, 0, 0, 0))
     relayout(5, put_to(r, 1, 1, 1))
     wait_all(halo_copies(1))
     both(lambda c: ghost_field(p, c, 1))
-    wait_all(k_copies())
+    wait_all([copies_z, copies_x, copies_y])
 
     def ghost_k(c):
-        def edge(cond, v):
-            return jnp.where(cond, 0.0, v)
         for yi in range(YI):
             v = kx[c, XI, yi]
             kx[c, 0, yi] = ghost_x(v, kxr[c], yi, True)
@@ -316,6 +317,14 @@
         v = ky[c, :, YI]
         ky[c, :, 0] = ghost_y(v, kyr[c], True)
         ky[c, :, YI] = edge(jnp.logical_and(sub == YB - 1, py == ny_dev - 1), v)
+
+        def diagonal(xi, _):
+            def line(yi):
+                v = s[c, xi, yi] + (kx[c, xi, yi] + kx[c, xi + 1, yi]) + (ky[c, xi, yi] + ky[c, xi, yi + 1])
+                s[c, xi, yi] = v + (kz[c, xi, yi, :ZI] + kz[c, xi, yi, 1:])
+            unrolled(YI, line)
+            return 0
+        lax.fori_loop(0, XI, diagonal, 0)
     both(ghost_k)
 
     for c in range(2):
@@ -374,7 +383,7 @@
         pltpu.make_async_copy(x.at[c], xo_hbm.at[c], out_sem.at[c]).wait()
 
 
-def cell_order(dims, x_hbm, hist_in, o_hbm, hist_out, x, stage, tmp, in_sem, out_sem):
+def cell_order(dims, x_hbm, hist_in, o_hbm, hist_out, x, stage, tmp, hist, in_sem, out_sem, hist_sem):
     XI, YI, ZI = dims
 
     def in_copy(c, xi):
@@ -382,11 +391,12 @@
 
     def out_copy(c, xi):
         return pltpu.make_async_copy(stage.at[c, :, xi], o_hbm.at[c, :, xi], out_sem.at[c, xi])
+    hist_copies = pltpu.make_async_copy(hist_in, hist, hist_sem.at[0]), pltpu.make_async_copy(hist, hist_out, hist_sem.at[1])
 
     for c in range(2):
         for xi in range(XI):
             in_copy(c, xi).start()
-    hist_out[...] = hist_in[...]
+    hist_copies[0].start()
     for c in range(2):
         def plane(xi, _):
             in_copy(c, xi).wait()
@@ -398,9 +408,13 @@
             out_copy(c, xi).start()
             return 0
         lax.fori_loop(0, XI, plane, 0)
+        if c == 0:
+            hist_copies[0].wait()
+            hist_copies[1].start()
     for c in range(2):
         for xi in range(XI):
             out_copy(c, xi).wait()
+    hist_copies[1].wait()
 
 
 def solution(mesh):
@@ -430,7 +444,7 @@
                 vregs(2, XI + 2, YI + 2, ZI + 2), vregs(2, XI + 2, YI + 2, ZI + 2),
                 vregs(2, XI, YI, ZI), vregs(2, XI, YI, ZI), vregs(2, XI, YI, ZI),
                 vregs(2, XI + 1, YI, ZI), vregs(2, XI, YI + 1, ZI), vregs(2, XI, YI, ZI + 1),
-                vregs(YI, ZI), pltpu.VMEM((ZI, ny, 128), f32),
+                pltpu.VMEM((ZI, ny, 128), f32),
                 vregs(2, 2, ZI), vregs(4, 2, 2, ZI), pltpu.VMEM((2, 2) + rows, f32), pltpu.VMEM((4, 2, 2) + rows, f32),
                 vregs(2, 2, mz), vregs(4, 2, 2, mz),
                 vregs(2, ZI), vregs(2, ZI), pltpu.VMEM((2,) + rows, f32), pltpu.VMEM((2,) + rows, f32),
@@ -444,14 +458,14 @@
             compiler_params=pltpu.CompilerParams(collective_id=0, has_side_effects=True, vmem_limit_bytes=67043328),
             name='cg',
         )(*args)
-        small = pl.BlockSpec(memory_space=pltpu.VMEM)
         x_out, hist = pl.pallas_call(
             functools.partial(cell_order, (XI, YI, ZI)),
             out_shape=(jax.ShapeDtypeStruct((2, XB, XI, nz, ny), f32), jax.ShapeDtypeStruct(hist.shape, f32)),
-            in_specs=[hbm, small], out_specs=(hbm, small),
+            in_specs=[hbm, hbm], out_specs=(hbm, hbm),
             scratch_shapes=[
                 vregs(2, XI, YI, ZI), pltpu.VMEM((2, XB, XI, nz, ny), f32), pltpu.VMEM((ZI, ny, 128), f32),
-                pltpu.SemaphoreType.DMA((2, XI)), pltpu.SemaphoreType.DMA((2, XI)),
+                pltpu.VMEM(hist.shape, f32),
+                pltpu.SemaphoreType.DMA((2, XI)), pltpu.SemaphoreType.DMA((2, XI)), pltpu.SemaphoreType.DMA((2,)),
             ],
             compiler_params=pltpu.CompilerParams(vmem_limit_bytes=67043328),
             name='cell_order',

time: 237 us -> 234 us (0.987)
  no operation moved by 1% of the time
where the time goes in v4:
time: 234 us
  Pallas kernels  234 us (100%)
    pallas_call x1, Pallas kernels, local_solve(): pl.pallas_call(functools.partial(kernel, sizes, (XI, YI, ZI, cells)), out...  230 us

profile of v4, /device:TPU:0, one launch (start us, length us, event | category | flops | bytes accessed | tf_op | source)
XLA Modules:
  0.0 234.2 jit_solution(2144601321328037389)
XLA Ops:
  0.6 229.8 %cg.1 = (f32[2,5,10,6,8,128]{5,4,3,2,1,0:T(8,128)}, f32[2,21]{1,0:T(2,128)}) custom-call(f32[2,16,5,48,80]{4,3,2,1,0:T(8,128)} %bitcast.21, f32[2,16,5,48,80]{4,3,2,1,0:T(8,128)} %bitcast.22, f32[2,16,5,48,80]{4,3,2,1,0:T(8,128)} %bitcast.23, f32[2,16,5,48,80]{4,3,2,1,0:T(8,128)} %bitcast.24, f32[2,16,5,48,80]{4,3,2,1,0:T(8,128)} %bitcast.25, ...), custom_call_target="tpu_custom_call" | custom-call | tf_op jit(solution)/shard_map/cg/pallas_call | solution.py:437
  230.5 3.7 %cell_order.1 = (f32[2,16,5,48,80]{4,3,2,1,0:T(8,128)}, f32[2,21]{1,0:T(2,128)}) custom-call(f32[2,5,10,6,8,128]{5,4,3,2,1,0:T(8,128)} %get-tuple-element.6.x_hbm, f32[2,21]{1,0:T(2,128)} %get-tuple-element.7.hist_in), custom_call_target="tpu_custom_call" | custom-call | tf_op jit(solution)/shard_map/cell_order/pallas_call | solution.py:461

commit v5 on v4

--- a/solution.py
+++ b/solution.py
@@ -45,17 +45,15 @@
         high = lax.div(2 * pos, size)
         return high * n + (1 - high) * (size - 1 - n)
 
+    others = []
+    for n in range(n_dev):
+        dev = (far_first(pz, nz_dev, n // (ny_dev * nx_dev)), far_first(py, ny_dev, n // nx_dev % ny_dev),
+               far_first(lax.div(px, 2), nx_dev // 2, n % nx_dev // 2) * 2 + n % 2)
+        others.append((dev, (dev[0] * ny_dev + dev[1]) * nx_dev + dev[2] != me))
+
     def each_other(fn):
-        def step(n, _):
-            dev = (far_first(pz, nz_dev, lax.div(n, ny_dev * nx_dev)),
-                   far_first(py, ny_dev, lax.rem(lax.div(n, nx_dev), ny_dev)),
-                   far_first(px, nx_dev, lax.rem(n, nx_dev)))
-
-            @pl.when((dev[0] * ny_dev + dev[1]) * nx_dev + dev[2] != me)
-            def _():
-                fn(dev)
-            return 0
-        lax.fori_loop(0, n_dev, step, 0, unroll=True)
+        for dev, is_other in others:
+            pl.when(is_other)(functools.partial(fn, dev))
 
     barrier = pltpu.get_barrier_semaphore()
     each_other(lambda dev: pl.semaphore_signal(barrier, inc=1, device_id=dev, device_id_type=MESH))
@@ -70,18 +68,27 @@
     xsl = slice(1, XI + 1)
     ytail = slice(min(YI, ZB) + 1, YI + 1)
 
+    def block(half, i):
+        n = half * (XI * ZI // 2) + i
+        return lax.div(n, ZI), lax.rem(n, ZI)
+
     def relayout(a, stores):
         def system(c, _):
             in_copy(a, c).wait()
 
-            def plane(xi, _):
-                def load(zi):
+            def chunk(half, _):
+                def load(i):
+                    xi, zi = block(half, i)
                     rows = stage[a, c, :, xi, pl.ds(zi, ZB, stride=ZI), :]
-                    tmp[zi] = rows.reshape(128, rows.shape[-1]).T
-                unrolled(ZI, load)
-                unrolled(ZI, lambda zi: unrolled(YI, lambda yi: stores(c, xi, yi, zi, tmp[zi, pl.ds(yi, YB, stride=YI), :])))
+                    tmp[i] = rows.reshape(128, rows.shape[-1]).T
+
+                def store(i):
+                    xi, zi = block(half, i)
+                    unrolled(YI, lambda yi: stores(c, xi, yi, zi, tmp[i, pl.ds(yi, YB, stride=YI), :]))
+                unrolled(XI * ZI // 2, load)
+                unrolled(XI * ZI // 2, store)
                 return 0
-            return lax.fori_loop(0, XI, plane, 0)
+            return lax.fori_loop(0, 2, chunk, 0)
         lax.fori_loop(0, 2, system, 0)
 
     def pack_x(get, shift, put):
@@ -398,16 +405,23 @@
             in_copy(c, xi).start()
     hist_copies[0].start()
     for c in range(2):
+        for xi in range(XI):
+            in_copy(c, xi).wait()
+
         def plane(xi, _):
-            in_copy(c, xi).wait()
-            for zi in range(ZI):
+            def gather(zi, _):
                 for yi in range(YI):
-                    tmp[zi, pl.ds(yi, YB, stride=YI), :] = x[c, xi, yi, zi]
-            for zi in range(ZI):
-                stage[c, :, xi, pl.ds(zi, ZB, stride=ZI), :] = tmp[zi].T.reshape(XB, ZB, tmp.shape[1])
+                    tmp[xi * ZI + zi, pl.ds(yi, YB, stride=YI), :] = x[c, xi, yi, zi]
+                return 0
+            lax.fori_loop(0, ZI, gather, 0, unroll=True)
+
+            def put(zi, _):
+                stage[c, :, xi, pl.ds(zi, ZB, stride=ZI), :] = tmp[xi * ZI + zi].T.reshape(XB, ZB, tmp.shape[1])
+                return 0
+            lax.fori_loop(0, ZI, put, 0, unroll=True)
             out_copy(c, xi).start()
             return 0
-        lax.fori_loop(0, XI, plane, 0)
+        lax.fori_loop(0, XI, plane, 0, unroll=True)
         if c == 0:
             hist_copies[0].wait()
             hist_copies[1].start()
@@ -444,7 +458,7 @@
                 vregs(2, XI + 2, YI + 2, ZI + 2), vregs(2, XI + 2, YI + 2, ZI + 2),
                 vregs(2, XI, YI, ZI), vregs(2, XI, YI, ZI), vregs(2, XI, YI, ZI),
                 vregs(2, XI + 1, YI, ZI), vregs(2, XI, YI + 1, ZI), vregs(2, XI, YI, ZI + 1),
-                pltpu.VMEM((ZI, ny, 128), f32),
+                pltpu.VMEM((XI * ZI // 2, ny, 128), f32),
                 vregs(2, 2, ZI), vregs(4, 2, 2, ZI), pltpu.VMEM((2, 2) + rows, f32), pltpu.VMEM((4, 2, 2) + rows, f32),
                 vregs(2, 2, mz), vregs(4, 2, 2, mz),
                 vregs(2, ZI), vregs(2, ZI), pltpu.VMEM((2,) + rows, f32), pltpu.VMEM((2,) + rows, f32),
@@ -463,7 +477,7 @@
             out_shape=(jax.ShapeDtypeStruct((2, XB, XI, nz, ny), f32), jax.ShapeDtypeStruct(hist.shape, f32)),
             in_specs=[hbm, hbm], out_specs=(hbm, hbm),
             scratch_shapes=[
-                vregs(2, XI, YI, ZI), pltpu.VMEM((2, XB, XI, nz, ny), f32), pltpu.VMEM((ZI, ny, 128), f32),
+                vregs(2, XI, YI, ZI), pltpu.VMEM((2, XB, XI, nz, ny), f32), pltpu.VMEM((XI * ZI, ny, 128), f32),
                 pltpu.VMEM(hist.shape, f32),
                 pltpu.SemaphoreType.DMA((2, XI)), pltpu.SemaphoreType.DMA((2, XI)), pltpu.SemaphoreType.DMA((2,)),
             ],

time: 234 us -> 232 us (level)
  no operation moved by 1% of the time
where the time goes in v5:
time: 232 us
  Pallas kernels  232 us (100%)
    pallas_call x1, Pallas kernels, local_solve(): pl.pallas_call(functools.partial(kernel, sizes, (XI, YI, ZI, cells)), out...  228 us

profile of v5, /device:TPU:0, one launch (start us, length us, event | category | flops | bytes accessed | tf_op | source)
XLA Modules:
  0.0 232.3 jit_solution(10607356136022999300)
XLA Ops:
  0.6 228.0 %cg.1 = (f32[2,5,10,6,8,128]{5,4,3,2,1,0:T(8,128)}, f32[2,21]{1,0:T(2,128)}) custom-call(f32[2,16,5,48,80]{4,3,2,1,0:T(8,128)} %bitcast.21, f32[2,16,5,48,80]{4,3,2,1,0:T(8,128)} %bitcast.22, f32[2,16,5,48,80]{4,3,2,1,0:T(8,128)} %bitcast.23, f32[2,16,5,48,80]{4,3,2,1,0:T(8,128)} %bitcast.24, f32[2,16,5,48,80]{4,3,2,1,0:T(8,128)} %bitcast.25, ...), custom_call_target="tpu_custom_call" | custom-call | tf_op jit(solution)/shard_map/cg/pallas_call | solution.py:451
  228.6 3.7 %cell_order.1 = (f32[2,16,5,48,80]{4,3,2,1,0:T(8,128)}, f32[2,21]{1,0:T(2,128)}) custom-call(f32[2,5,10,6,8,128]{5,4,3,2,1,0:T(8,128)} %get-tuple-element.6.x_hbm, f32[2,21]{1,0:T(2,128)} %get-tuple-element.7.hist_in), custom_call_target="tpu_custom_call" | custom-call | tf_op jit(solution)/shard_map/cell_order/pallas_call | solution.py:475

commit v6 on v5

--- a/solution.py
+++ b/solution.py
@@ -34,7 +34,7 @@
     def in_copy(a, c):
         return pltpu.make_async_copy(arrays[a].at[c], stage.at[a, c], in_sem.at[a, c])
 
-    for a in range(6):
+    for a in (0, 3, 1, 2, 4, 5):
         for c in range(2):
             in_copy(a, c).start()
 

time: 232 us -> 231 us (level)
  no operation moved by 1% of the time
where the time goes in v6:
time: 231 us
  Pallas kernels  230 us (100%)
    pallas_call x1, Pallas kernels, local_solve(): pl.pallas_call(functools.partial(kernel, sizes, (XI, YI, ZI, cells)), out...  227 us

profile of v6, /device:TPU:0, one launch (start us, length us, event | category | flops | bytes accessed | tf_op | source)
XLA Modules:
  0.0 230.9 jit_solution(955002604740372313)
XLA Ops:
  0.6 226.6 %cg.1 = (f32[2,5,10,6,8,128]{5,4,3,2,1,0:T(8,128)}, f32[2,21]{1,0:T(2,128)}) custom-call(f32[2,16,5,48,80]{4,3,2,1,0:T(8,128)} %bitcast.21, f32[2,16,5,48,80]{4,3,2,1,0:T(8,128)} %bitcast.22, f32[2,16,5,48,80]{4,3,2,1,0:T(8,128)} %bitcast.23, f32[2,16,5,48,80]{4,3,2,1,0:T(8,128)} %bitcast.24, f32[2,16,5,48,80]{4,3,2,1,0:T(8,128)} %bitcast.25, ...), custom_call_target="tpu_custom_call" | custom-call | tf_op jit(solution)/shard_map/cg/pallas_call | solution.py:451
  227.2 3.7 %cell_order.1 = (f32[2,16,5,48,80]{4,3,2,1,0:T(8,128)}, f32[2,21]{1,0:T(2,128)}) custom-call(f32[2,5,10,6,8,128]{5,4,3,2,1,0:T(8,128)} %get-tuple-element.6.x_hbm, f32[2,21]{1,0:T(2,128)} %get-tuple-element.7.hist_in), custom_call_target="tpu_custom_call" | custom-call | tf_op jit(solution)/shard_map/cell_order/pallas_call | solution.py:475
